TPU v7x, 256 devices: a whole 4x4x8 slice. The times are simulated.
256 devices in a mesh: seq: 64 (over x, z, core), head: 4 (over y).
Axes of the slice: x: 4, y: 4, z: 8, core: 2. Of those that a mesh axis runs over, the one named last changes fastest.
Arguments:
- queries: bfloat16 [32768, 1024], P('seq', 'head'), may hold values from -6 to 6
- key_vectors: bfloat16 [32768, 1024], P('seq', 'head'), may hold values from -6 to 6
- values: bfloat16 [32768, 2048], P('seq', 'head'), may hold values from -6 to 6
- log_gate: bfloat16 [32768, 1024], P('seq', 'head'), may hold values from -1.6 to 0, as said below
- out_gate: bfloat16 [32768, 2048], P('seq', 'head'), may hold values from -6 to 6
- norm_gain: float32 [2048], P('head'), may hold values from 0.5 to 1.5
- out_weight: bfloat16 [2048, 2048], P('head'), may hold values from -0.1875 to 0.1875
Outputs:
- mixed: bfloat16 [32768, 2048], P('seq', 'head')
Inputs may be any that keep to these rules, and one draw needn't show every extreme that they name: `log_gate`: every entry is below zero.
All inputs are finite; a program needn't handle non-finite values.
Results may differ from a plain program's by a relative error of at most 0.017.
Values may be sent and summed in bfloat16 or wider, within the bound.
No kernel may reach another device: no remote copies, remote signals or barrier semaphores. Data moves between devices by JAX's collectives and lax.ppermute only.
A program may use at most 128 MiB of HBM per device.

v0:
```python
import jax
import jax.numpy as jnp
from jax import lax
from jax.experimental import pallas as pl
from jax.experimental.pallas import tpu as pltpu
from jax.sharding import Mesh
from jax.sharding import PartitionSpec as P


DK = 256
DV = 512
SPAN = 64
LANE = 128
SEQ = ("chip_x", "chip_z", "core")
CHIPS = ("chip_x", "chip_z")
F32 = jnp.float32
BF16 = jnp.bfloat16
VMEM = pl.BlockSpec(memory_space=pltpu.VMEM)
HBM = pl.BlockSpec(memory_space=pltpu.HBM)


def call(body, outs, *args, fetched=(), scratch=(), copies=0, outs_in=VMEM):
    moved = sum(a.size * a.dtype.itemsize for a in args)
    args = [
        pltpu.with_memory_space_constraint(a, pltpu.HBM) if i in fetched else a
        for i, a in enumerate(args)
    ]
    if fetched and not copies:
        scratch = [pltpu.VMEM(args[i].shape, args[i].dtype) for i in fetched]
        copies = len(fetched)
    if copies:
        scratch = [*scratch, pltpu.SemaphoreType.DMA((copies,))]
    return pl.pallas_call(
        body,
        out_shape=outs,
        in_specs=[HBM if i in fetched else VMEM for i in range(len(args))],
        out_specs=jax.tree.map(lambda _: outs_in, outs),
        scratch_shapes=scratch,
        cost_estimate=pl.CostEstimate(flops=10**9, transcendentals=0, bytes_accessed=moved),
        compiler_params=pltpu.CompilerParams(vmem_limit_bytes=16 * 2**20),
    )(*args)


def dot(a, b, dims=((1,), (0,))):
    return lax.dot_general(a, b, (dims, ((), ())), preferred_element_type=F32)


def triangle(length, keep):
    row = lax.broadcasted_iota(jnp.int32, (length, length), 0)
    col = lax.broadcasted_iota(jnp.int32, (length, length), 1)
    return jnp.where(keep(row, col), 1.0, 0.0).astype(BF16)


def stacked(*parts):
    row = lax.broadcasted_iota(jnp.int32, (8, LANE), 0)
    block = jnp.zeros((8, LANE), F32)
    for at, part in enumerate(parts):
        block = jnp.where(row == at, part, block)
    return block


def split_bf16(values):
    high = values.astype(BF16).astype(F32)
    return high, values - high


def fetch(sems, *pairs):
    copies = [pltpu.make_async_copy(src, dst, sems.at[i]) for i, (src, dst) in enumerate(pairs)]
    for copy in copies:
        copy.start()
    return copies


def columns(index, width):
    return pl.ds(pl.multiple_of(index * width, width), width)


def head_columns(shift, width):
    count = lax.axis_size("head")
    return columns(lax.rem(lax.axis_index("head") + shift, count), width)


def swap_body(k_hbm, v_hbm, g_hbm, swap_ref, log_ref, state_ref, k_ref, v_ref, g_ref, sems):
    gate_copy, k_copy, v_copy = fetch(sems, (g_hbm, g_ref), (k_hbm, k_ref), (v_hbm, v_ref))
    length = k_ref.shape[0]
    half = DV // 2
    mask = triangle(length, lambda r, c: c > r)
    gate_copy.wait()
    gate = g_ref[...]
    after = dot(mask, gate)
    total = after[0:1] + gate[0:1].astype(F32)
    k_copy.wait()
    k_state = (k_ref[...].astype(F32) * jnp.exp(after)).astype(BF16)
    state_ref[...] = k_state
    v_copy.wait()
    theirs = columns(1 - lax.axis_index("core"), half)
    state = dot(v_ref[:, theirs], k_state, ((0,), (0,))).astype(BF16)
    swap_ref[0:half, :] = state[:, :LANE]
    swap_ref[half : 2 * half, :] = state[:, LANE:]
    left_high, left_low = split_bf16(total[:, :LANE])
    right_high, right_low = split_bf16(total[:, LANE:])
    tail = stacked(left_high, right_high, left_low, right_low)
    swap_ref[2 * half :, :] = jnp.concatenate([tail, tail], axis=0).astype(BF16)
    log_ref[...] = stacked(total[:, :LANE], total[:, LANE:])


def own_body(v_hbm, state_ref, own_ref, v_ref, sems):
    (copy,) = fetch(sems, (v_hbm, v_ref))
    copy.wait()
    half = DV // 2
    mine = columns(lax.axis_index("core"), half)
    state = dot(v_ref[:, mine], state_ref[...], ((0,), (0,)))
    own_ref[0:half, :] = state[:, :LANE]
    own_ref[half:, :] = state[:, LANE:]


def join_body(own_ref, log_ref, swap_ref, out_ref, first_ref, decay_ref):
    pieces, rows = (out_ref.shape[0], (out_ref.shape[1] - 8) // 2)
    half = pieces * rows
    early = lax.axis_index("core") == 0
    tail = swap_ref[2 * half : 2 * half + 8, :].astype(F32)
    sums = []
    decays = []
    for side in range(2):
        at = slice(side * half, (side + 1) * half)
        own_log = log_ref[side : side + 1, :]
        other_log = tail[side : side + 1] + tail[side + 2 : side + 3]
        own = own_ref[at, :]
        other = swap_ref[at, :].astype(F32)
        first = jnp.where(early, own, other)
        second = jnp.where(early, other, own)
        state = first * jnp.exp(jnp.where(early, other_log, own_log)) + second
        first_ref[at, :] = first.astype(BF16)
        decays.append(jnp.exp(jnp.where(early, own_log, other_log)))
        sums.append(own_log + other_log)
        piece = slice(side * rows, (side + 1) * rows)
        out_ref[:, piece, :] = state.reshape(pieces, rows, LANE).astype(BF16)
    decay_ref[...] = stacked(*decays)
    left_high, left_low = split_bf16(sums[0])
    right_high, right_low = split_bf16(sums[1])
    tail = stacked(left_high, right_high, left_low, right_low)
    out_ref[:, 2 * rows :, :] = jnp.broadcast_to(tail[None], (pieces, 8, LANE)).astype(BF16)


def scan_body(in_ref, out_ref):
    pieces, rows = (in_ref.shape[0], out_ref.shape[1] // 2)
    left = right = jnp.zeros((rows, LANE), F32)
    for j in range(pieces):
        out_ref[j, 0:rows, :] = left.astype(BF16)
        out_ref[j, rows : 2 * rows, :] = right.astype(BF16)
        tail = in_ref[j, 2 * rows :, :].astype(F32)
        left = left * jnp.exp(tail[0:1] + tail[2:3]) + in_ref[j, 0:rows, :].astype(F32)
        right = right * jnp.exp(tail[1:2] + tail[3:4]) + in_ref[j, rows : 2 * rows, :].astype(F32)


def part_body(in_ref, first_ref, decay_ref, keep_ref, send_ref):
    pieces, rows = (in_ref.shape[0], in_ref.shape[1] // 2)
    half = pieces * rows
    early = lax.axis_index("core") == 0
    for side in range(2):
        at = slice(side * half, (side + 1) * half)
        piece = slice(side * rows, (side + 1) * rows)
        entering = in_ref[:, piece, :].astype(F32).reshape(half, LANE)
        between = entering * decay_ref[side : side + 1, :] + first_ref[at, :].astype(F32)
        keep_ref[at, :] = jnp.where(early, entering, between).astype(BF16)
        send_ref[at, :] = jnp.where(early, between, entering).astype(BF16)


def local_body(
    q_hbm, k_hbm, v_hbm, g_hbm, outer_hbm, w_hbm, gain_ref,
    att_ref, start_ref, scale_ref, w_ref, q_ref, k_ref, v_ref, g_ref, outer_ref, sems,
):
    far_columns = w_hbm.at[:, head_columns(2, w_ref.shape[1])]
    *copies, far_copy = fetch(
        sems,
        (g_hbm, g_ref),
        (q_hbm, q_ref),
        (k_hbm, k_ref),
        (v_hbm, v_ref),
        (outer_hbm, outer_ref),
        (far_columns, w_ref),
    )
    length = q_ref.shape[0]
    lower = triangle(SPAN, lambda r, c: c <= r)
    row = lax.broadcasted_iota(jnp.int32, (SPAN, SPAN), 0)
    col = lax.broadcasted_iota(jnp.int32, (SPAN, SPAN), 1)
    for copy in copies:
        copy.wait()
    carried = None
    before = jnp.zeros((1, DK), F32)
    for i in range(length // SPAN):
        at = slice(i * SPAN, (i + 1) * SPAN)
        running = dot(lower, g_ref[at, :])
        middle = running[SPAN // 2 : SPAN // 2 + 1]
        ending = running[SPAN - 1 : SPAN]
        query_f = q_ref[at, :].astype(F32)
        key_f = k_ref[at, :].astype(F32)
        value = v_ref[at, :]
        q_inter = query_f * jnp.exp(running)
        q_intra = (query_f * jnp.exp(running - middle)).astype(BF16)
        k_intra = (key_f * jnp.exp(middle - running)).astype(BF16)
        scores = dot(q_intra, k_intra, ((1,), (1,)))
        weights = jnp.where(col <= row, scores, 0.0).astype(BF16)
        attention = dot(weights, value)
        if i:
            attention = attention + dot(q_inter.astype(BF16), carried.astype(BF16))
        att_ref[at, :] = attention
        start_ref[at, :] = (query_f * jnp.exp(running + before)).astype(BF16)
        before = before + ending
        if (i + 1) * SPAN < length:
            k_state = (key_f * jnp.exp(ending - running)).T.astype(BF16)
            block = dot(k_state, value)
            carried = block if i == 0 else carried * jnp.exp(ending).reshape(DK, 1) + block
        outer_f = outer_ref[at, :].astype(F32)
        scale = outer_f / (1.0 + jnp.exp(-outer_f)) * gain_ref[...]
        scale_ref[at, :] = scale.astype(BF16)
    far_copy.wait()


def keep_body(keep_ref, q_ref, att_ref, out_ref, square_ref):
    half = keep_ref.shape[0] // 2
    attention = att_ref[:, columns(lax.axis_index("core"), half)]
    attention = attention + dot(q_ref[:, :LANE], keep_ref[:half, :], ((1,), (1,)))
    attention = attention + dot(q_ref[:, LANE:], keep_ref[half:, :], ((1,), (1,)))
    out_ref[...] = attention
    square_ref[...] = jnp.sum(attention * attention, axis=-1, keepdims=True)


def finish_body(
    other_ref, q_ref, att_ref, kept_ref, square_ref, scale_ref, w_ref,
    gated_ref, far_up_ref, far_down_ref,
):
    half = other_ref.shape[0] // 2
    core = lax.axis_index("core")
    here, there = columns(core, half), columns(1 - core, half)
    attention = att_ref[:, there]
    attention = attention + dot(q_ref[:, :LANE], other_ref[:half, :], ((1,), (1,)))
    attention = attention + dot(q_ref[:, LANE:], other_ref[half:, :], ((1,), (1,)))
    total = square_ref[...] + jnp.sum(attention * attention, axis=-1, keepdims=True)
    inverse = lax.rsqrt(total * (1.0 / DV) + 1e-05)
    gated_ref[:, there] = (attention * inverse * scale_ref[:, there].astype(F32)).astype(BF16)
    gated_ref[:, here] = (kept_ref[...] * inverse * scale_ref[:, here].astype(F32)).astype(BF16)
    split = far_up_ref.shape[0]
    far_up_ref[...] = dot(gated_ref[:split, :], w_ref[...]).astype(BF16)
    far_down_ref[...] = dot(gated_ref[split:, :], w_ref[...]).astype(BF16)


def fetch_columns(w_hbm, w_ref, sems, *shifts):
    width = w_ref.shape[-1]
    pairs = [(w_hbm.at[:, head_columns(s, width)], w_ref.at[i]) for i, s in enumerate(shifts)]
    return fetch(sems, *pairs)


def direct_body(gated_ref, w_hbm, up_ref, down_ref, w_ref, sems):
    copies = fetch_columns(w_hbm, w_ref, sems, 1, 3)
    length, split = (gated_ref.shape[0], down_ref.shape[0])
    copies[0].wait()
    up_ref[...] = dot(gated_ref[length - up_ref.shape[0] :, :], w_ref[0]).astype(BF16)
    copies[1].wait()
    down_ref[...] = dot(gated_ref[:split, :], w_ref[1]).astype(BF16)


def near_body(gated_ref, w_hbm, up_ref, down_ref, own_ref, w_ref, sems):
    copies = fetch_columns(w_hbm, w_ref, sems, 1, 3, 0)
    split = up_ref.shape[0]
    copies[0].wait()
    up_ref[...] = dot(gated_ref[:split, :], w_ref[0])
    copies[1].wait()
    down_ref[...] = dot(gated_ref[split:, :], w_ref[1])
    copies[2].wait()
    own_ref[...] = dot(gated_ref[...], w_ref[2])


def pass_body(up_ref, down_ref, far_up_ref, far_down_ref, up_out_ref, down_out_ref):
    up_out_ref[...] = (up_ref[...] + far_up_ref[...].astype(F32)).astype(BF16)
    down_out_ref[...] = (down_ref[...] + far_down_ref[...].astype(F32)).astype(BF16)


def sum_body(own_ref, below_a_ref, below_b_ref, above_a_ref, above_b_ref, out_ref):
    split = below_a_ref.shape[0]
    for at, below, above in (
        (slice(0, split), below_a_ref, above_a_ref),
        (slice(split, own_ref.shape[0]), below_b_ref, above_b_ref),
    ):
        total = own_ref[at, :] + below[...].astype(F32) + above[...].astype(F32)
        out_ref[at, :] = total.astype(BF16)


def ring(axis, shift):
    length = lax.axis_size(axis)
    return [(i, (i + shift) % length) for i in range(length)]


def shards(queries, key_vectors, values, log_gate, out_gate, norm_gain, out_weight):
    length = queries.shape[0]
    pieces = lax.axis_size(CHIPS)
    half = DV // 2
    rows = half // pieces
    width = out_weight.shape[1] // lax.axis_size("head")
    shape = jax.ShapeDtypeStruct
    small = shape((8, LANE), F32)
    swap, own_log, k_state = call(
        swap_body,
        (shape((DV + 16, LANE), BF16), small, shape((length, DK), BF16)),
        key_vectors,
        values,
        log_gate,
        fetched=(0, 1, 2),
    )
    swapped = lax.ppermute(swap, "core", ring("core", 1))
    own = call(own_body, shape((DV, LANE), F32), values, k_state, fetched=(0,))
    sent, early, decay = call(
        join_body,
        (shape((pieces, 2 * rows + 8, LANE), BF16), shape((DV, LANE), BF16), small),
        own,
        own_log,
        swapped,
    )
    slices = lax.all_to_all(sent, CHIPS, 0, 0, tiled=True)
    prefixes = call(scan_body, shape((pieces, 2 * rows, LANE), BF16), slices)
    prefixes, queries = lax.optimization_barrier((prefixes, queries))
    inputs = (queries, key_vectors, values, log_gate, out_gate)
    att_local, q_start, scale, w_far = call(
        local_body,
        (
            shape((length, DV), F32),
            shape((length, DK), BF16),
            shape((length, DV), BF16),
            shape((DV, width), BF16),
        ),
        *inputs,
        out_weight,
        norm_gain.reshape(1, DV),
        fetched=(0, 1, 2, 3, 4, 5),
        scratch=[pltpu.VMEM(part.shape, BF16) for part in inputs],
        copies=6,
    )
    entering = lax.all_to_all(prefixes, CHIPS, 0, 0, tiled=True)
    state_half = shape((DV, LANE), BF16)
    entering, att_local, q_start, scale, w_far = lax.optimization_barrier(
        (entering, att_local, q_start, scale, w_far)
    )
    keep, send = call(part_body, (state_half, state_half), entering, early, decay)
    other = lax.ppermute(send, "core", ring("core", 1))
    kept, square = call(
        keep_body, (shape((length, half), F32), shape((length, 1), F32)), keep, q_start, att_local
    )
    split = length // 2
    first, last = shape((split, width), BF16), shape((length - split, width), BF16)
    gated, far_up, far_down = call(
        finish_body,
        (shape((length, DV), BF16), first, last),
        other,
        q_start,
        att_local,
        kept,
        square,
        scale,
        w_far,
    )
    up, down = ring("head", 1), ring("head", -1)
    far_up = lax.ppermute(far_up, "head", up)
    far_down = lax.ppermute(far_down, "head", down)
    up_b, down_a = call(
        direct_body,
        (last, first),
        gated,
        out_weight,
        fetched=(1,),
        scratch=[pltpu.VMEM((2, DV, width), BF16)],
        copies=2,
    )
    below_b = lax.ppermute(up_b, "head", up)
    above_a = lax.ppermute(down_a, "head", down)
    up_a, down_b, own_part = call(
        near_body,
        (shape(first.shape, F32), shape(last.shape, F32), shape((length, width), F32)),
        gated,
        out_weight,
        fetched=(1,),
        scratch=[pltpu.VMEM((3, DV, width), BF16)],
        copies=3,
    )
    up_a, down_b = call(pass_body, (first, last), up_a, down_b, far_up, far_down)
    below_a = lax.ppermute(up_a, "head", up)
    above_b = lax.ppermute(down_b, "head", down)
    return call(
        sum_body, shape((length, width), BF16), own_part, below_a, below_b, above_a, above_b
    )


def solution(mesh):
    split = Mesh(mesh.devices.reshape(4, 8, 2, mesh.shape["head"]), (*SEQ, "head"))
    in_specs = (
        P(SEQ, "head"),
        P(SEQ, "head"),
        P(SEQ, "head"),
        P(SEQ, "head"),
        P(SEQ, "head"),
        P("head"),
        P("head", None),
    )
    out_specs = P(SEQ, "head")

    return jax.shard_map(
        shards, mesh=split, in_specs=in_specs, out_specs=out_specs, check_vma=False
    )
```

profile of v0, /device:TPU:24, one launch (start us, length us, event | category | flops | bytes accessed | tf_op | source)
XLA Modules:
  0.0 66.2 jit_solution(13501345915198808122)
XLA Ops:
  0.0 1.8 %shard_map.73 = (bf16[528,128]{1,0:T(8,128)(2,1)S(1)}, f32[8,128]{1,0:T(8,128)S(1)}, bf16[512,256]{1,0:T(8,128)(2,1)S(1)}) custom-call(bf16[512,256]{1,0:T(8,128)(2,1)} %k_hbm.3, bf16[512,512]{1,0:T(8,128)(2,1)} %v_hbm.5, bf16[512,256]{1,0:T(8,128)(2,1)} %g_hbm.3), custom_call_target="tpu_custom_call" | custom-call | flops 1000000000 | bytes 1048576 | tf_op jit(solution)/shard_map/pallas_call | solution.py:33
  1.9 1.3 %shard_map.74.own_ref = f32[512,128]{1,0:T(8,128)S(1)} custom-call(bf16[512,512]{1,0:T(8,128)(2,1)} %v_hbm.5, bf16[512,256]{1,0:T(8,128)(2,1)S(1)} %get-tuple-element.36.state_ref), custom_call_target="tpu_custom_call" | custom-call | flops 1000000000 | bytes 786432 | tf_op jit(solution)/shard_map/pallas_call | solution.py:33
  3.3 23.3 %all_to_all.10.in_ref = bf16[32,24,128]{2,1,0:T(8,128)(2,1)S(1)} all-to-all(bf16[32,24,128]{2,1,0:T(8,128)(2,1)S(1)} %get-tuple-element.39), channel_id=1, replica_groups=mesh['chip_x'=4,'chip_z'=8,'core'=2,'head'=4] {'chip_x','chip_z'}, dimensions={0} | all-to-all | bytes 393216 | tf_op jit(solution)/shard_map/all_to_all | solution.py:319
  26.7 0.7 %shard_map.76 = bf16[32,16,128]{2,1,0:T(8,128)(2,1)} custom-call(bf16[32,24,128]{2,1,0:T(8,128)(2,1)S(1)} %all_to_all.10.in_ref), custom_call_target="tpu_custom_call" | custom-call | flops 1000000000 | bytes 196608 | tf_op jit(solution)/shard_map/pallas_call | solution.py:33
  27.4 3.9 %all-to-all-start.1 = ((bf16[32,16,128]{2,1,0:T(8,128)(2,1)}), bf16[32,16,128]{2,1,0:T(8,128)(2,1)S(1)}, u32[]{:S(2)}, u32[]{:S(2)}) async-start(bf16[32,16,128]{2,1,0:T(8,128)(2,1)} %shard_map.76), calls=%async_computation.1 | async-start | bytes 262144 | tf_op jit(solution)/shard_map/all_to_all | solution.py:338
  31.3 4.8 %shard_map.77 = (f32[512,512]{1,0:T(8,128)S(1)}, bf16[512,256]{1,0:T(8,128)(2,1)S(1)}, bf16[512,512]{1,0:T(8,128)(2,1)S(1)}, bf16[512,512]{1,0:T(8,128)(2,1)S(1)}) custom-call(bf16[512,256]{1,0:T(8,128)(2,1)} %q_hbm, bf16[512,256]{1,0:T(8,128)(2,1)} %k_hbm.3, bf16[512,512]{1,0:T(8,128)(2,1)} %v_hbm.5, bf16[512,256]{1,0:T(8,128)(2,1)} %g_hbm.3, ...), custom_call_target="tpu_custom_call" | custom-call | flops 1000000000 | bytes 3934208 | tf_op jit(solution)/shard_map/pallas_call | solution.py:33
  36.1 5.4 %all-to-all-done.1.in_ref = bf16[32,16,128]{2,1,0:T(8,128)(2,1)S(1)} async-done(((bf16[32,16,128]{2,1,0:T(8,128)(2,1)}), bf16[32,16,128]{2,1,0:T(8,128)(2,1)S(1)}, u32[]{:S(2)}, u32[]{:S(2)}) %all-to-all-start.1) | async-done | bytes 131104 | tf_op jit(solution)/shard_map/all_to_all | solution.py:338
  41.8 0.4 shard_map.79
  42.1 1.0 %collective-permute-done.1.other_ref = bf16[512,128]{1,0:T(8,128)(2,1)S(1)} collective-permute-done((bf16[512,128]{1,0:T(8,128)(2,1)S(1)}, bf16[512,128]{1,0:T(8,128)(2,1)S(1)}, u32[]{:S(2)}, u32[]{:S(2)}) %collective-permute-start.1) | collective-permute-done | bytes 131104 | tf_op jit(solution)/shard_map/ppermute | solution.py:344
  43.1 1.2 %shard_map.80 = (bf16[512,512]{1,0:T(8,128)(2,1)S(1)}, bf16[256,512]{1,0:T(8,128)(2,1)S(1)}, bf16[256,512]{1,0:T(8,128)(2,1)S(1)}) custom-call(bf16[512,128]{1,0:T(8,128)(2,1)S(1)} %collective-permute-done.1.other_ref, bf16[512,256]{1,0:T(8,128)(2,1)S(1)} %get-tuple-element.50.q_ref, f32[512,512]{1,0:T(8,128)S(1)} %get-tuple-element.51.att_ref, ...), custom_call_target="tpu_custom_call" | custom-call | flops 1000000000 | bytes 3016704 | tf_op jit(solution)/shard_map/pallas_call | solution.py:33
  44.6 1.8 %collective-permute-start.3 = (bf16[256,512]{1,0:T(8,128)(2,1)S(1)}, bf16[256,512]{1,0:T(8,128)(2,1)S(1)}, u32[]{:S(2)}, u32[]{:S(2)}) collective-permute-start(bf16[256,512]{1,0:T(8,128)(2,1)S(1)} %get-tuple-element.62), channel_id=1, source_target_pairs={{0,3},{1,0},{2,1},{3,2},{4,7},{5,4},{6,5},{7,6},{8,11},{9,8},{10,9... | collective-permute-start | bytes 786440 | tf_op jit(solution)/shard_map/ppermute | solution.py:363
  46.4 1.7 %shard_map.83 = (bf16[256,512]{1,0:T(8,128)(2,1)S(1)}, bf16[256,512]{1,0:T(8,128)(2,1)S(1)}) custom-call(bf16[512,512]{1,0:T(8,128)(2,1)S(1)} %get-tuple-element.57.gated_ref, bf16[512,2048]{1,0:T(8,128)(2,1)} %w_hbm.5), custom_call_target="tpu_custom_call" | custom-call | flops 1000000000 | bytes 2621440 | tf_op jit(solution)/shard_map/pallas_call | solution.py:33
  48.1 1.5 %collective-permute-start.5 = (bf16[256,512]{1,0:T(8,128)(2,1)S(1)}, bf16[256,512]{1,0:T(8,128)(2,1)S(1)}, u32[]{:S(2)}, u32[]{:S(2)}) collective-permute-start(bf16[256,512]{1,0:T(8,128)(2,1)S(1)} %get-tuple-element.64), channel_id=1, source_target_pairs={{0,1},{1,2},{2,3},{3,0},{4,5},{5,6},{6,7},{7,4},{8,9},{9,10},{10,1... | collective-permute-start | bytes 786440 | tf_op jit(solution)/shard_map/ppermute | solution.py:373
  49.6 0.6 collective-permute-start.6
  50.2 2.1 %shard_map.81 = (f32[256,512]{1,0:T(8,128)S(1)}, f32[256,512]{1,0:T(8,128)S(1)}, f32[512,512]{1,0:T(8,128)S(1)}) custom-call(bf16[512,512]{1,0:T(8,128)(2,1)S(1)} %get-tuple-element.57.gated_ref, bf16[512,2048]{1,0:T(8,128)(2,1)} %w_hbm.5), custom_call_target="tpu_custom_call" | custom-call | flops 1000000000 | bytes 2621440 | tf_op jit(solution)/shard_map/pallas_call | solution.py:33
  52.3 1.3 %collective-permute-done.2.far_up_ref = bf16[256,512]{1,0:T(8,128)(2,1)S(1)} collective-permute-done((bf16[256,512]{1,0:T(8,128)(2,1)S(1)}, bf16[256,512]{1,0:T(8,128)(2,1)S(1)}, u32[]{:S(2)}, u32[]{:S(2)}) %collective-permute-start.2) | collective-permute-done | bytes 262176 | tf_op jit(solution)/shard_map/ppermute | solution.py:362
  53.5 1.4 %collective-permute-done.3.far_down_ref = bf16[256,512]{1,0:T(8,128)(2,1)S(1)} collective-permute-done((bf16[256,512]{1,0:T(8,128)(2,1)S(1)}, bf16[256,512]{1,0:T(8,128)(2,1)S(1)}, u32[]{:S(2)}, u32[]{:S(2)}) %collective-permute-start.3) | collective-permute-done | bytes 262176 | tf_op jit(solution)/shard_map/ppermute | solution.py:363
  55.1 0.4 collective-permute-start.4
  55.5 1.7 %collective-permute-start.7 = (bf16[256,512]{1,0:T(8,128)(2,1)S(1)}, bf16[256,512]{1,0:T(8,128)(2,1)S(1)}, u32[]{:S(2)}, u32[]{:S(2)}) collective-permute-start(bf16[256,512]{1,0:T(8,128)(2,1)S(1)} %get-tuple-element.66), channel_id=1, source_target_pairs={{0,3},{1,0},{2,1},{3,2},{4,7},{5,4},{6,5},{7,6},{8,11},{9,8},{10,9... | collective-permute-start | bytes 786440 | tf_op jit(solution)/shard_map/ppermute | solution.py:386
  57.2 2.0 %collective-permute-done.5.below_b_ref = bf16[256,512]{1,0:T(8,128)(2,1)S(1)} collective-permute-done((bf16[256,512]{1,0:T(8,128)(2,1)S(1)}, bf16[256,512]{1,0:T(8,128)(2,1)S(1)}, u32[]{:S(2)}, u32[]{:S(2)}) %collective-permute-start.5) | collective-permute-done | bytes 262176 | tf_op jit(solution)/shard_map/ppermute | solution.py:373
  59.2 1.4 %collective-permute-done.6.above_a_ref = bf16[256,512]{1,0:T(8,128)(2,1)S(1)} collective-permute-done((bf16[256,512]{1,0:T(8,128)(2,1)S(1)}, bf16[256,512]{1,0:T(8,128)(2,1)S(1)}, u32[]{:S(2)}, u32[]{:S(2)}) %collective-permute-start.6) | collective-permute-done | bytes 262176 | tf_op jit(solution)/shard_map/ppermute | solution.py:374
  60.6 3.4 %collective-permute-done.4.below_a_ref = bf16[256,512]{1,0:T(8,128)(2,1)S(1)} collective-permute-done((bf16[256,512]{1,0:T(8,128)(2,1)S(1)}, bf16[256,512]{1,0:T(8,128)(2,1)S(1)}, u32[]{:S(2)}, u32[]{:S(2)}) %collective-permute-start.4) | collective-permute-done | bytes 262176 | tf_op jit(solution)/shard_map/ppermute | solution.py:385
  64.0 1.3 %collective-permute-done.7.above_b_ref = bf16[256,512]{1,0:T(8,128)(2,1)S(1)} collective-permute-done((bf16[256,512]{1,0:T(8,128)(2,1)S(1)}, bf16[256,512]{1,0:T(8,128)(2,1)S(1)}, u32[]{:S(2)}, u32[]{:S(2)}) %collective-permute-start.7) | collective-permute-done | bytes 262176 | tf_op jit(solution)/shard_map/ppermute | solution.py:386
  65.3 0.9 %shard_map.84 = bf16[512,512]{1,0:T(8,128)(2,1)} custom-call(f32[512,512]{1,0:T(8,128)S(1)} %get-tuple-element.58.own_ref, bf16[256,512]{1,0:T(8,128)(2,1)S(1)} %collective-permute-done.4.below_a_ref, bf16[256,512]{1,0:T(8,128)(2,1)S(1)} %collective-permute-done.5.below_b_ref, bf16[256,512]{1,0:T(8,128)(2,1)S(1)} %collective-permute-done.6.above_a_ref, ...), custom_call_target="tpu_custom_call" | custom-call | flops 1000000000 | bytes 2097152 | tf_op jit(solution)/shard_map/pallas_call | solution.py:33
  (9 shorter events, 0.7 us)
Async XLA Ops:
  1.8 1.4 %collective-permute-start = (bf16[528,128]{1,0:T(8,128)(2,1)S(1)}, bf16[528,128]{1,0:T(8,128)(2,1)S(1)}, u32[]{:S(2)}, u32[]{:S(2)}) collective-permute-start(bf16[528,128]{1,0:T(8,128)(2,1)S(1)} %get-tuple-element.38), channel_id=1, source_target_pairs={{0,4},{4,0},{1,5},{5,1},{2,6},{6,2},{3,7},{7,3},{8,12},{12,8},{9,1... | collective-permute-start | bytes 405512 | tf_op jit(solution)/shard_map/ppermute | solution.py:310
  3.3 28.0 %copy-start = (f32[512]{0:T(512)S(1)}, f32[512]{0:T(512)}, u32[]{:S(2)}) copy-start(f32[512]{0:T(512)} %param.12) | copy-start | bytes 6148
  27.4 14.2 %all-to-all-start.1 = ((bf16[32,16,128]{2,1,0:T(8,128)(2,1)}), bf16[32,16,128]{2,1,0:T(8,128)(2,1)S(1)}, u32[]{:S(2)}, u32[]{:S(2)}) async-start(bf16[32,16,128]{2,1,0:T(8,128)(2,1)} %shard_map.76), calls=%async_computation.1 | async-start | bytes 262144 | tf_op jit(solution)/shard_map/all_to_all | solution.py:338
  41.7 1.4 %collective-permute-start.1 = (bf16[512,128]{1,0:T(8,128)(2,1)S(1)}, bf16[512,128]{1,0:T(8,128)(2,1)S(1)}, u32[]{:S(2)}, u32[]{:S(2)}) collective-permute-start(bf16[512,128]{1,0:T(8,128)(2,1)S(1)} %get-tuple-element.49), channel_id=1, source_target_pairs={{0,4},{4,0},{1,5},{5,1},{2,6},{6,2},{3,7},{7,3},{8,12},{12,8},{9,1... | collective-permute-start | bytes 393224 | tf_op jit(solution)/shard_map/ppermute | solution.py:344
  44.3 9.3 %collective-permute-start.2 = (bf16[256,512]{1,0:T(8,128)(2,1)S(1)}, bf16[256,512]{1,0:T(8,128)(2,1)S(1)}, u32[]{:S(2)}, u32[]{:S(2)}) collective-permute-start(bf16[256,512]{1,0:T(8,128)(2,1)S(1)} %get-tuple-element.61), channel_id=1, source_target_pairs={{0,1},{1,2},{2,3},{3,0},{4,5},{5,6},{6,7},{7,4},{8,9},{9,10},{10,1... | collective-permute-start | bytes 786440 | tf_op jit(solution)/shard_map/ppermute | solution.py:362
  44.6 10.4 %collective-permute-start.3 = (bf16[256,512]{1,0:T(8,128)(2,1)S(1)}, bf16[256,512]{1,0:T(8,128)(2,1)S(1)}, u32[]{:S(2)}, u32[]{:S(2)}) collective-permute-start(bf16[256,512]{1,0:T(8,128)(2,1)S(1)} %get-tuple-element.62), channel_id=1, source_target_pairs={{0,3},{1,0},{2,1},{3,2},{4,7},{5,4},{6,5},{7,6},{8,11},{9,8},{10,9... | collective-permute-start | bytes 786440 | tf_op jit(solution)/shard_map/ppermute | solution.py:363
  48.1 11.1 %collective-permute-start.5 = (bf16[256,512]{1,0:T(8,128)(2,1)S(1)}, bf16[256,512]{1,0:T(8,128)(2,1)S(1)}, u32[]{:S(2)}, u32[]{:S(2)}) collective-permute-start(bf16[256,512]{1,0:T(8,128)(2,1)S(1)} %get-tuple-element.64), channel_id=1, source_target_pairs={{0,1},{1,2},{2,3},{3,0},{4,5},{5,6},{6,7},{7,4},{8,9},{9,10},{10,1... | collective-permute-start | bytes 786440 | tf_op jit(solution)/shard_map/ppermute | solution.py:373
  49.6 11.0 %collective-permute-start.6 = (bf16[256,512]{1,0:T(8,128)(2,1)S(1)}, bf16[256,512]{1,0:T(8,128)(2,1)S(1)}, u32[]{:S(2)}, u32[]{:S(2)}) collective-permute-start(bf16[256,512]{1,0:T(8,128)(2,1)S(1)} %get-tuple-element.65), channel_id=1, source_target_pairs={{0,3},{1,0},{2,1},{3,2},{4,7},{5,4},{6,5},{7,6},{8,11},{9,8},{10,9... | collective-permute-start | bytes 786440 | tf_op jit(solution)/shard_map/ppermute | solution.py:374
  55.1 8.9 %collective-permute-start.4 = (bf16[256,512]{1,0:T(8,128)(2,1)S(1)}, bf16[256,512]{1,0:T(8,128)(2,1)S(1)}, u32[]{:S(2)}, u32[]{:S(2)}) collective-permute-start(bf16[256,512]{1,0:T(8,128)(2,1)S(1)} %get-tuple-element.63), channel_id=1, source_target_pairs={{0,1},{1,2},{2,3},{3,0},{4,5},{5,6},{6,7},{7,4},{8,9},{9,10},{10,1... | collective-permute-start | bytes 786440 | tf_op jit(solution)/shard_map/ppermute | solution.py:385
  55.5 9.8 %collective-permute-start.7 = (bf16[256,512]{1,0:T(8,128)(2,1)S(1)}, bf16[256,512]{1,0:T(8,128)(2,1)S(1)}, u32[]{:S(2)}, u32[]{:S(2)}) collective-permute-start(bf16[256,512]{1,0:T(8,128)(2,1)S(1)} %get-tuple-element.66), channel_id=1, source_target_pairs={{0,3},{1,0},{2,1},{3,2},{4,7},{5,4},{6,5},{7,6},{8,11},{9,8},{10,9... | collective-permute-start | bytes 786440 | tf_op jit(solution)/shard_map/ppermute | solution.py:386
where the time goes:
time: 66.8 us; the launch traced here: 66.2 us
  blocking collectives  23.3 us (35%)
  waiting for transfers between devices  17.2 us (26%)
  Pallas kernels  15.2 us (23%)
  starting transfers between devices  10.4 us (16%)
    all_to_all x1, blocking collectives, shards(): slices = lax.all_to_all(sent, CHIPS, 0, 0, tiled=True)  23.3 us
    pallas_call x12, Pallas kernels, call(): pl.pallas_call(body, out_shape=outs, in_specs=[HBM if i in fetched else V...  15.2 us
    all_to_all x1, waiting for transfers between devices, shards(): entering = lax.all_to_all(prefixes, CHIPS, 0, 0, tiled=True)  5.44 us
    all_to_all x1, starting transfers between devices, shards(): entering = lax.all_to_all(prefixes, CHIPS, 0, 0, tiled=True)  3.91 us
    ppermute x1, waiting for transfers between devices, shards(): below_a = lax.ppermute(up_a, 'head', up)  3.36 us
    ppermute x1, waiting for transfers between devices, shards(): below_b = lax.ppermute(up_b, 'head', up)  1.99 us
    ppermute x1, starting transfers between devices, shards(): far_down = lax.ppermute(far_down, 'head', down)  1.81 us
    ppermute x1, starting transfers between devices, shards(): above_b = lax.ppermute(down_b, 'head', down)  1.67 us
  transfers between devices with their start and end apart: 9, of which 8 were waited for; matrix products, arithmetic and copies ran while one was open for 0% of the time, Pallas kernels for 16%

commit v1 on v0

--- a/solution.py
+++ b/solution.py
@@ -227,8 +227,7 @@
 
 
 def finish_body(
-    other_ref, q_ref, att_ref, kept_ref, square_ref, scale_ref, w_ref,
-    gated_ref, far_up_ref, far_down_ref,
+    other_ref, q_ref, att_ref, kept_ref, square_ref, scale_ref, w_ref, gated_ref, far_ref
 ):
     half = other_ref.shape[0] // 2
     core = lax.axis_index("core")
@@ -240,50 +239,40 @@
     inverse = lax.rsqrt(total * (1.0 / DV) + 1e-05)
     gated_ref[:, there] = (attention * inverse * scale_ref[:, there].astype(F32)).astype(BF16)
     gated_ref[:, here] = (kept_ref[...] * inverse * scale_ref[:, here].astype(F32)).astype(BF16)
-    split = far_up_ref.shape[0]
-    far_up_ref[...] = dot(gated_ref[:split, :], w_ref[...]).astype(BF16)
-    far_down_ref[...] = dot(gated_ref[split:, :], w_ref[...]).astype(BF16)
-
-
-def fetch_columns(w_hbm, w_ref, sems, *shifts):
-    width = w_ref.shape[-1]
-    pairs = [(w_hbm.at[:, head_columns(s, width)], w_ref.at[i]) for i, s in enumerate(shifts)]
-    return fetch(sems, *pairs)
-
-
-def direct_body(gated_ref, w_hbm, up_ref, down_ref, w_ref, sems):
-    copies = fetch_columns(w_hbm, w_ref, sems, 1, 3)
-    length, split = (gated_ref.shape[0], down_ref.shape[0])
-    copies[0].wait()
-    up_ref[...] = dot(gated_ref[length - up_ref.shape[0] :, :], w_ref[0]).astype(BF16)
-    copies[1].wait()
-    down_ref[...] = dot(gated_ref[:split, :], w_ref[1]).astype(BF16)
-
-
-def near_body(gated_ref, w_hbm, up_ref, down_ref, own_ref, w_ref, sems):
-    copies = fetch_columns(w_hbm, w_ref, sems, 1, 3, 0)
-    split = up_ref.shape[0]
-    copies[0].wait()
-    up_ref[...] = dot(gated_ref[:split, :], w_ref[0])
-    copies[1].wait()
-    down_ref[...] = dot(gated_ref[split:, :], w_ref[1])
-    copies[2].wait()
-    own_ref[...] = dot(gated_ref[...], w_ref[2])
-
-
-def pass_body(up_ref, down_ref, far_up_ref, far_down_ref, up_out_ref, down_out_ref):
-    up_out_ref[...] = (up_ref[...] + far_up_ref[...].astype(F32)).astype(BF16)
-    down_out_ref[...] = (down_ref[...] + far_down_ref[...].astype(F32)).astype(BF16)
-
-
-def sum_body(own_ref, below_a_ref, below_b_ref, above_a_ref, above_b_ref, out_ref):
-    split = below_a_ref.shape[0]
-    for at, below, above in (
-        (slice(0, split), below_a_ref, above_a_ref),
-        (slice(split, own_ref.shape[0]), below_b_ref, above_b_ref),
-    ):
-        total = own_ref[at, :] + below[...].astype(F32) + above[...].astype(F32)
-        out_ref[at, :] = total.astype(BF16)
+    far_ref[...] = dot(gated_ref[...], w_ref[...]).astype(BF16)
+
+
+def onward():
+    return jnp.where(lax.axis_index("core") == 0, 1, lax.axis_size("head") - 1)
+
+
+def direct_body(gated_ref, w_hbm, out_ref, w_ref, sems):
+    back = head_columns(lax.axis_size("head") - onward(), w_ref.shape[1])
+    (copy,) = fetch(sems, (w_hbm.at[:, back], w_ref))
+    copy.wait()
+    out_ref[...] = dot(gated_ref[...], w_ref[...]).astype(BF16)
+
+
+def near_body(gated_ref, w_hbm, onward_ref, own_ref, w_onward_ref, w_own_ref, sems):
+    width = w_own_ref.shape[1]
+    onward_copy, own_copy = fetch(
+        sems,
+        (w_hbm.at[:, head_columns(onward(), width)], w_onward_ref),
+        (w_hbm.at[:, head_columns(0, width)], w_own_ref),
+    )
+    onward_copy.wait()
+    onward_ref[...] = dot(gated_ref[...], w_onward_ref[...])
+    own_copy.wait()
+    own_ref[...] = dot(gated_ref[...], w_own_ref[...])
+
+
+def pass_body(onward_ref, far_ref, out_ref):
+    out_ref[...] = (onward_ref[...] + far_ref[...].astype(F32)).astype(BF16)
+
+
+def sum_body(own_ref, direct_ref, passed_ref, out_ref):
+    total = own_ref[...] + direct_ref[...].astype(F32) + passed_ref[...].astype(F32)
+    out_ref[...] = total.astype(BF16)
 
 
 def ring(axis, shift):
@@ -345,11 +334,11 @@
     kept, square = call(
         keep_body, (shape((length, half), F32), shape((length, 1), F32)), keep, q_start, att_local
     )
-    split = length // 2
-    first, last = shape((split, width), BF16), shape((length - split, width), BF16)
-    gated, far_up, far_down = call(
+    block = shape((length, width), BF16)
+    block_f = shape((length, width), F32)
+    gated, far = call(
         finish_body,
-        (shape((length, DV), BF16), first, last),
+        (shape((length, DV), BF16), block),
         other,
         q_start,
         att_local,
@@ -358,35 +347,27 @@
         scale,
         w_far,
     )
-    up, down = ring("head", 1), ring("head", -1)
-    far_up = lax.ppermute(far_up, "head", up)
-    far_down = lax.ppermute(far_down, "head", down)
-    up_b, down_a = call(
-        direct_body,
-        (last, first),
+    heads = lax.axis_size("head")
+    way = [(c * heads + y, c * heads + (y + 1 - 2 * c) % heads) for c in (0, 1) for y in range(heads)]
+    against = [(target, source) for source, target in way]
+    group = ("core", "head")
+    far = lax.ppermute(far, group, way)
+    column = pltpu.VMEM((DV, width), BF16)
+    direct = call(
+        direct_body, block, gated, out_weight, fetched=(1,), scratch=[column], copies=1
+    )
+    direct = lax.ppermute(direct, group, against)
+    passed, own_part = call(
+        near_body,
+        (block_f, block_f),
         gated,
         out_weight,
         fetched=(1,),
-        scratch=[pltpu.VMEM((2, DV, width), BF16)],
+        scratch=[column, column],
         copies=2,
     )
-    below_b = lax.ppermute(up_b, "head", up)
-    above_a = lax.ppermute(down_a, "head", down)
-    up_a, down_b, own_part = call(
-        near_body,
-        (shape(first.shape, F32), shape(last.shape, F32), shape((length, width), F32)),
-        gated,
-        out_weight,
-        fetched=(1,),
-        scratch=[pltpu.VMEM((3, DV, width), BF16)],
-        copies=3,
-    )
-    up_a, down_b = call(pass_body, (first, last), up_a, down_b, far_up, far_down)
-    below_a = lax.ppermute(up_a, "head", up)
-    above_b = lax.ppermute(down_b, "head", down)
-    return call(
-        sum_body, shape((length, width), BF16), own_part, below_a, below_b, above_a, above_b
-    )
+    passed = lax.ppermute(call(pass_body, block, passed, far), group, way)
+    return call(sum_body, block, own_part, direct, passed)
 
 
 def solution(mesh):

time: 66.8 us -> 68.8 us (1.030)
  waiting for transfers between devices: 17.2 us -> 23.6 us
  starting transfers between devices: 10.4 us -> 6.36 us
    ppermute x6 -> x3, waiting for transfers between devices: 10.8 us -> 17.2 us  [the longest x1 8.04 us: shards(): far = lax.ppermute(far, group, way)]
    ppermute x6 -> x3, starting transfers between devices: 6.31 us -> 2.26 us  [the longest x1 1.88 us: shards(): direct = lax.ppermute(direct, group, against)]
  transfers between devices with their start and end apart: 9 -> 6, of which waited for: 8 -> 5; matrix products, arithmetic and copies ran while one was open for 0% -> 0% of each run, Pallas kernels for 16% -> 15%
where the time goes in v1:
time: 68.8 us; the launch traced here: 68.1 us
  waiting for transfers between devices  23.6 us (34%)
  blocking collectives  23.3 us (34%)
  Pallas kernels  14.7 us (21%)
  starting transfers between devices  6.36 us (9%)
    all_to_all x1, blocking collectives, shards(): slices = lax.all_to_all(sent, CHIPS, 0, 0, tiled=True)  23.3 us
    pallas_call x12, Pallas kernels, call(): pl.pallas_call(body, out_shape=outs, in_specs=[HBM if i in fetched else V...  14.7 us
    ppermute x1, waiting for transfers between devices, shards(): far = lax.ppermute(far, group, way)  8.04 us
    ppermute x1, waiting for transfers between devices, shards(): passed = lax.ppermute(call(pass_body, block, passed, far), group, way)  7.74 us
    all_to_all x1, waiting for transfers between devices, shards(): entering = lax.all_to_all(prefixes, CHIPS, 0, 0, tiled=True)  5.44 us
    all_to_all x1, starting transfers between devices, shards(): entering = lax.all_to_all(prefixes, CHIPS, 0, 0, tiled=True)  3.91 us
    ppermute x1, starting transfers between devices, shards(): direct = lax.ppermute(direct, group, against)  1.88 us
    ppermute x1, waiting for transfers between devices, shards(): direct = lax.ppermute(direct, group, against)  1.42 us
  transfers between devices with their start and end apart: 6, of which 5 were waited for; matrix products, arithmetic and copies ran while one was open for 0% of the time, Pallas kernels for 15%

profile of v1, /device:TPU:24, one launch (start us, length us, event | category | flops | bytes accessed | tf_op | source)
XLA Modules:
  0.0 68.1 jit_solution(14918048520586562472)
XLA Ops:
  0.0 1.8 %shard_map.73 = (bf16[528,128]{1,0:T(8,128)(2,1)S(1)}, f32[8,128]{1,0:T(8,128)S(1)}, bf16[512,256]{1,0:T(8,128)(2,1)S(1)}) custom-call(bf16[512,256]{1,0:T(8,128)(2,1)} %k_hbm.3, bf16[512,512]{1,0:T(8,128)(2,1)} %v_hbm.5, bf16[512,256]{1,0:T(8,128)(2,1)} %g_hbm.3), custom_call_target="tpu_custom_call" | custom-call | flops 1000000000 | bytes 1048576 | tf_op jit(solution)/shard_map/pallas_call | solution.py:33
  1.8 0.1 collective-permute-start
  1.9 1.3 %shard_map.74.own_ref = f32[512,128]{1,0:T(8,128)S(1)} custom-call(bf16[512,512]{1,0:T(8,128)(2,1)} %v_hbm.5, bf16[512,256]{1,0:T(8,128)(2,1)S(1)} %get-tuple-element.30.state_ref), custom_call_target="tpu_custom_call" | custom-call | flops 1000000000 | bytes 786432 | tf_op jit(solution)/shard_map/pallas_call | solution.py:33
  3.2 0.1 shard_map.75
  3.3 23.3 %all_to_all.10.in_ref = bf16[32,24,128]{2,1,0:T(8,128)(2,1)S(1)} all-to-all(bf16[32,24,128]{2,1,0:T(8,128)(2,1)S(1)} %get-tuple-element.33), channel_id=1, replica_groups=mesh['chip_x'=4,'chip_z'=8,'core'=2,'head'=4] {'chip_x','chip_z'}, dimensions={0} | all-to-all | bytes 393216 | tf_op jit(solution)/shard_map/all_to_all | solution.py:308
  26.7 0.7 %shard_map.76 = bf16[32,16,128]{2,1,0:T(8,128)(2,1)} custom-call(bf16[32,24,128]{2,1,0:T(8,128)(2,1)S(1)} %all_to_all.10.in_ref), custom_call_target="tpu_custom_call" | custom-call | flops 1000000000 | bytes 196608 | tf_op jit(solution)/shard_map/pallas_call | solution.py:33
  27.4 3.9 %all-to-all-start.1 = ((bf16[32,16,128]{2,1,0:T(8,128)(2,1)}), bf16[32,16,128]{2,1,0:T(8,128)(2,1)S(1)}, u32[]{:S(2)}, u32[]{:S(2)}) async-start(bf16[32,16,128]{2,1,0:T(8,128)(2,1)} %shard_map.76), calls=%async_computation.1 | async-start | bytes 262144 | tf_op jit(solution)/shard_map/all_to_all | solution.py:327
  31.3 4.8 %shard_map.77 = (f32[512,512]{1,0:T(8,128)S(1)}, bf16[512,256]{1,0:T(8,128)(2,1)S(1)}, bf16[512,512]{1,0:T(8,128)(2,1)S(1)}, bf16[512,512]{1,0:T(8,128)(2,1)S(1)}) custom-call(bf16[512,256]{1,0:T(8,128)(2,1)} %q_hbm, bf16[512,256]{1,0:T(8,128)(2,1)} %k_hbm.3, bf16[512,512]{1,0:T(8,128)(2,1)} %v_hbm.5, bf16[512,256]{1,0:T(8,128)(2,1)} %g_hbm.3, ...), custom_call_target="tpu_custom_call" | custom-call | flops 1000000000 | bytes 3934208 | tf_op jit(solution)/shard_map/pallas_call | solution.py:33
  36.1 5.4 %all-to-all-done.1.in_ref = bf16[32,16,128]{2,1,0:T(8,128)(2,1)S(1)} async-done(((bf16[32,16,128]{2,1,0:T(8,128)(2,1)}), bf16[32,16,128]{2,1,0:T(8,128)(2,1)S(1)}, u32[]{:S(2)}, u32[]{:S(2)}) %all-to-all-start.1) | async-done | bytes 131104 | tf_op jit(solution)/shard_map/all_to_all | solution.py:327
  41.6 0.1 shard_map.78
  41.7 0.1 collective-permute-start.1
  41.8 0.4 shard_map.79
  42.1 1.0 %collective-permute-done.1.other_ref = bf16[512,128]{1,0:T(8,128)(2,1)S(1)} collective-permute-done((bf16[512,128]{1,0:T(8,128)(2,1)S(1)}, bf16[512,128]{1,0:T(8,128)(2,1)S(1)}, u32[]{:S(2)}, u32[]{:S(2)}) %collective-permute-start.1) | collective-permute-done | bytes 131104 | tf_op jit(solution)/shard_map/ppermute | solution.py:333
  43.1 1.1 %shard_map.80 = (bf16[512,512]{1,0:T(8,128)(2,1)S(1)}, bf16[512,512]{1,0:T(8,128)(2,1)S(1)}) custom-call(bf16[512,128]{1,0:T(8,128)(2,1)S(1)} %collective-permute-done.1.other_ref, bf16[512,256]{1,0:T(8,128)(2,1)S(1)} %get-tuple-element.44.q_ref, f32[512,512]{1,0:T(8,128)S(1)} %get-tuple-element.45.att_ref, f32[512,256]{1,0:T(8,128)S(1)} %get-tuple-element.47.kept_ref, ...), custom_call_target="tpu_custom_call" | custom-call | flops 1000000000 | bytes 3016704 | tf_op jit(solution)/shard_map/pallas_call | solution.py:33
  44.2 0.3 collective-permute-start.3
  44.5 1.5 %shard_map.82 = bf16[512,512]{1,0:T(8,128)(2,1)S(1)} custom-call(bf16[512,512]{1,0:T(8,128)(2,1)S(1)} %get-tuple-element.51.gated_ref, bf16[512,2048]{1,0:T(8,128)(2,1)} %w_hbm.5), custom_call_target="tpu_custom_call" | custom-call | flops 1000000000 | bytes 2621440 | tf_op jit(solution)/shard_map/pallas_call | solution.py:33
  46.0 1.9 %collective-permute-start.2 = (bf16[512,512]{1,0:T(8,128)(2,1)S(1)}, bf16[512,512]{1,0:T(8,128)(2,1)S(1)}, u32[]{:S(2)}, u32[]{:S(2)}) collective-permute-start(bf16[512,512]{1,0:T(8,128)(2,1)S(1)} %shard_map.82), channel_id=1, source_target_pairs={{1,0},{2,1},{3,2},{0,3},{7,4},{4,5},{5,6},{6,7},{9,8},{10,9},{11,1... | collective-permute-start | bytes 1572872 | tf_op jit(solution)/shard_map/ppermute | solution.py:359
  47.8 1.9 %shard_map.81 = (f32[512,512]{1,0:T(8,128)S(1)}, f32[512,512]{1,0:T(8,128)S(1)}) custom-call(bf16[512,512]{1,0:T(8,128)(2,1)S(1)} %get-tuple-element.51.gated_ref, bf16[512,2048]{1,0:T(8,128)(2,1)} %w_hbm.5), custom_call_target="tpu_custom_call" | custom-call | flops 1000000000 | bytes 2621440 | tf_op jit(solution)/shard_map/pallas_call | solution.py:33
  49.8 8.0 %collective-permute-done.3.far_ref = bf16[512,512]{1,0:T(8,128)(2,1)S(1)} collective-permute-done((bf16[512,512]{1,0:T(8,128)(2,1)S(1)}, bf16[512,512]{1,0:T(8,128)(2,1)S(1)}, u32[]{:S(2)}, u32[]{:S(2)}) %collective-permute-start.3) | collective-permute-done | bytes 524320 | tf_op jit(solution)/shard_map/ppermute | solution.py:354
  57.8 0.1 shard_map.83
  57.9 0.1 collective-permute-start.4
  58.0 1.4 %collective-permute-done.2.direct_ref = bf16[512,512]{1,0:T(8,128)(2,1)S(1)} collective-permute-done((bf16[512,512]{1,0:T(8,128)(2,1)S(1)}, bf16[512,512]{1,0:T(8,128)(2,1)S(1)}, u32[]{:S(2)}, u32[]{:S(2)}) %collective-permute-start.2) | collective-permute-done | bytes 524320 | tf_op jit(solution)/shard_map/ppermute | solution.py:359
  59.4 7.7 %collective-permute-done.4.passed_ref = bf16[512,512]{1,0:T(8,128)(2,1)S(1)} collective-permute-done((bf16[512,512]{1,0:T(8,128)(2,1)S(1)}, bf16[512,512]{1,0:T(8,128)(2,1)S(1)}, u32[]{:S(2)}, u32[]{:S(2)}) %collective-permute-start.4) | collective-permute-done | bytes 524320 | tf_op jit(solution)/shard_map/ppermute | solution.py:369
  67.2 0.9 %shard_map.84 = bf16[512,512]{1,0:T(8,128)(2,1)} custom-call(f32[512,512]{1,0:T(8,128)S(1)} %get-tuple-element.52.own_ref, bf16[512,512]{1,0:T(8,128)(2,1)S(1)} %collective-permute-done.2.direct_ref, bf16[512,512]{1,0:T(8,128)(2,1)S(1)} %collective-permute-done.4.passed_ref), custom_call_target="tpu_custom_call" | custom-call | flops 1000000000 | bytes 2097152 | tf_op jit(solution)/shard_map/pallas_call | solution.py:33
  (3 shorter events, 0.0 us)
Async XLA Ops:
  1.8 1.4 %collective-permute-start = (bf16[528,128]{1,0:T(8,128)(2,1)S(1)}, bf16[528,128]{1,0:T(8,128)(2,1)S(1)}, u32[]{:S(2)}, u32[]{:S(2)}) collective-permute-start(bf16[528,128]{1,0:T(8,128)(2,1)S(1)} %get-tuple-element.32), channel_id=1, source_target_pairs={{0,4},{4,0},{1,5},{5,1},{2,6},{6,2},{3,7},{7,3},{8,12},{12,8},{9,1... | collective-permute-start | bytes 405512 | tf_op jit(solution)/shard_map/ppermute | solution.py:299
  3.3 28.0 %copy-start = (f32[512]{0:T(512)S(1)}, f32[512]{0:T(512)}, u32[]{:S(2)}) copy-start(f32[512]{0:T(512)} %param.12) | copy-start | bytes 6148
  27.4 14.2 %all-to-all-start.1 = ((bf16[32,16,128]{2,1,0:T(8,128)(2,1)}), bf16[32,16,128]{2,1,0:T(8,128)(2,1)S(1)}, u32[]{:S(2)}, u32[]{:S(2)}) async-start(bf16[32,16,128]{2,1,0:T(8,128)(2,1)} %shard_map.76), calls=%async_computation.1 | async-start | bytes 262144 | tf_op jit(solution)/shard_map/all_to_all | solution.py:327
  41.7 1.4 %collective-permute-start.1 = (bf16[512,128]{1,0:T(8,128)(2,1)S(1)}, bf16[512,128]{1,0:T(8,128)(2,1)S(1)}, u32[]{:S(2)}, u32[]{:S(2)}) collective-permute-start(bf16[512,128]{1,0:T(8,128)(2,1)S(1)} %get-tuple-element.43), channel_id=1, source_target_pairs={{0,4},{4,0},{1,5},{5,1},{2,6},{6,2},{3,7},{7,3},{8,12},{12,8},{9,1... | collective-permute-start | bytes 393224 | tf_op jit(solution)/shard_map/ppermute | solution.py:333
  44.2 13.7 %collective-permute-start.3 = (bf16[512,512]{1,0:T(8,128)(2,1)S(1)}, bf16[512,512]{1,0:T(8,128)(2,1)S(1)}, u32[]{:S(2)}, u32[]{:S(2)}) collective-permute-start(bf16[512,512]{1,0:T(8,128)(2,1)S(1)} %get-tuple-element.54), channel_id=1, source_target_pairs={{0,1},{1,2},{2,3},{3,0},{4,7},{5,4},{6,5},{7,6},{8,9},{9,10},{10,1... | collective-permute-start | bytes 1572872 | tf_op jit(solution)/shard_map/ppermute | solution.py:354
  46.0 13.5 %collective-permute-start.2 = (bf16[512,512]{1,0:T(8,128)(2,1)S(1)}, bf16[512,512]{1,0:T(8,128)(2,1)S(1)}, u32[]{:S(2)}, u32[]{:S(2)}) collective-permute-start(bf16[512,512]{1,0:T(8,128)(2,1)S(1)} %shard_map.82), channel_id=1, source_target_pairs={{1,0},{2,1},{3,2},{0,3},{7,4},{4,5},{5,6},{6,7},{9,8},{10,9},{11,1... | collective-permute-start | bytes 1572872 | tf_op jit(solution)/shard_map/ppermute | solution.py:359
  57.9 9.3 %collective-permute-start.4 = (bf16[512,512]{1,0:T(8,128)(2,1)S(1)}, bf16[512,512]{1,0:T(8,128)(2,1)S(1)}, u32[]{:S(2)}, u32[]{:S(2)}) collective-permute-start(bf16[512,512]{1,0:T(8,128)(2,1)S(1)} %shard_map.83), channel_id=1, source_target_pairs={{0,1},{1,2},{2,3},{3,0},{4,7},{5,4},{6,5},{7,6},{8,9},{9,10},{10,1... | collective-permute-start | bytes 1572872 | tf_op jit(solution)/shard_map/ppermute | solution.py:369

commit v2 on v1

--- a/solution.py
+++ b/solution.py
@@ -353,9 +353,7 @@
     group = ("core", "head")
     far = lax.ppermute(far, group, way)
     column = pltpu.VMEM((DV, width), BF16)
-    direct = call(
-        direct_body, block, gated, out_weight, fetched=(1,), scratch=[column], copies=1
-    )
+    direct = call(direct_body, block, gated, out_weight, fetched=(1,), scratch=[column], copies=1)
     direct = lax.ppermute(direct, group, against)
     passed, own_part = call(
         near_body,
@@ -366,7 +364,8 @@
         scratch=[column, column],
         copies=2,
     )
-    passed = lax.ppermute(call(pass_body, block, passed, far), group, way)
+    passed = call(pass_body, block, passed, far)
+    passed = lax.ppermute(passed, group, way)
     return call(sum_body, block, own_part, direct, passed)
 
 

time: 68.8 us -> 68.8 us (level)
  no operation moved by 1% of the time
where the time goes in v2:
time: 68.8 us; the launch traced here: 68.1 us
  waiting for transfers between devices  23.6 us (34%)
  blocking collectives  23.3 us (34%)
  Pallas kernels  14.7 us (21%)
  starting transfers between devices  6.36 us (9%)
    all_to_all x1, blocking collectives, shards(): slices = lax.all_to_all(sent, CHIPS, 0, 0, tiled=True)  23.3 us
    pallas_call x12, Pallas kernels, call(): pl.pallas_call(body, out_shape=outs, in_specs=[HBM if i in fetched else V...  14.7 us
    ppermute x1, waiting for transfers between devices, shards(): far = lax.ppermute(far, group, way)  8.04 us
    ppermute x1, waiting for transfers between devices, shards(): passed = lax.ppermute(passed, group, way)  7.74 us
    all_to_all x1, waiting for transfers between devices, shards(): entering = lax.all_to_all(prefixes, CHIPS, 0, 0, tiled=True)  5.44 us
    all_to_all x1, starting transfers between devices, shards(): entering = lax.all_to_all(prefixes, CHIPS, 0, 0, tiled=True)  3.91 us
    ppermute x1, starting transfers between devices, shards(): direct = lax.ppermute(direct, group, against)  1.88 us
    ppermute x1, waiting for transfers between devices, shards(): direct = lax.ppermute(direct, group, against)  1.42 us
  transfers between devices with their start and end apart: 6, of which 5 were waited for; matrix products, arithmetic and copies ran while one was open for 0% of the time, Pallas kernels for 15%

profile of v2, /device:TPU:24, one launch (start us, length us, event | category | flops | bytes accessed | tf_op | source)
XLA Modules:
  0.0 68.1 jit_solution(14918048520586562472)
XLA Ops:
  0.0 1.8 %shard_map.73 = (bf16[528,128]{1,0:T(8,128)(2,1)S(1)}, f32[8,128]{1,0:T(8,128)S(1)}, bf16[512,256]{1,0:T(8,128)(2,1)S(1)}) custom-call(bf16[512,256]{1,0:T(8,128)(2,1)} %k_hbm.3, bf16[512,512]{1,0:T(8,128)(2,1)} %v_hbm.5, bf16[512,256]{1,0:T(8,128)(2,1)} %g_hbm.3), custom_call_target="tpu_custom_call" | custom-call | flops 1000000000 | bytes 1048576 | tf_op jit(solution)/shard_map/pallas_call | solution.py:33
  1.8 0.1 collective-permute-start
  1.9 1.3 %shard_map.74.own_ref = f32[512,128]{1,0:T(8,128)S(1)} custom-call(bf16[512,512]{1,0:T(8,128)(2,1)} %v_hbm.5, bf16[512,256]{1,0:T(8,128)(2,1)S(1)} %get-tuple-element.30.state_ref), custom_call_target="tpu_custom_call" | custom-call | flops 1000000000 | bytes 786432 | tf_op jit(solution)/shard_map/pallas_call | solution.py:33
  3.2 0.1 shard_map.75
  3.3 23.3 %all_to_all.10.in_ref = bf16[32,24,128]{2,1,0:T(8,128)(2,1)S(1)} all-to-all(bf16[32,24,128]{2,1,0:T(8,128)(2,1)S(1)} %get-tuple-element.33), channel_id=1, replica_groups=mesh['chip_x'=4,'chip_z'=8,'core'=2,'head'=4] {'chip_x','chip_z'}, dimensions={0} | all-to-all | bytes 393216 | tf_op jit(solution)/shard_map/all_to_all | solution.py:308
  26.7 0.7 %shard_map.76 = bf16[32,16,128]{2,1,0:T(8,128)(2,1)} custom-call(bf16[32,24,128]{2,1,0:T(8,128)(2,1)S(1)} %all_to_all.10.in_ref), custom_call_target="tpu_custom_call" | custom-call | flops 1000000000 | bytes 196608 | tf_op jit(solution)/shard_map/pallas_call | solution.py:33
  27.4 3.9 %all-to-all-start.1 = ((bf16[32,16,128]{2,1,0:T(8,128)(2,1)}), bf16[32,16,128]{2,1,0:T(8,128)(2,1)S(1)}, u32[]{:S(2)}, u32[]{:S(2)}) async-start(bf16[32,16,128]{2,1,0:T(8,128)(2,1)} %shard_map.76), calls=%async_computation.1 | async-start | bytes 262144 | tf_op jit(solution)/shard_map/all_to_all | solution.py:327
  31.3 4.8 %shard_map.77 = (f32[512,512]{1,0:T(8,128)S(1)}, bf16[512,256]{1,0:T(8,128)(2,1)S(1)}, bf16[512,512]{1,0:T(8,128)(2,1)S(1)}, bf16[512,512]{1,0:T(8,128)(2,1)S(1)}) custom-call(bf16[512,256]{1,0:T(8,128)(2,1)} %q_hbm, bf16[512,256]{1,0:T(8,128)(2,1)} %k_hbm.3, bf16[512,512]{1,0:T(8,128)(2,1)} %v_hbm.5, bf16[512,256]{1,0:T(8,128)(2,1)} %g_hbm.3, ...), custom_call_target="tpu_custom_call" | custom-call | flops 1000000000 | bytes 3934208 | tf_op jit(solution)/shard_map/pallas_call | solution.py:33
  36.1 5.4 %all-to-all-done.1.in_ref = bf16[32,16,128]{2,1,0:T(8,128)(2,1)S(1)} async-done(((bf16[32,16,128]{2,1,0:T(8,128)(2,1)}), bf16[32,16,128]{2,1,0:T(8,128)(2,1)S(1)}, u32[]{:S(2)}, u32[]{:S(2)}) %all-to-all-start.1) | async-done | bytes 131104 | tf_op jit(solution)/shard_map/all_to_all | solution.py:327
  41.6 0.1 shard_map.78
  41.7 0.1 collective-permute-start.1
  41.8 0.4 shard_map.79
  42.1 1.0 %collective-permute-done.1.other_ref = bf16[512,128]{1,0:T(8,128)(2,1)S(1)} collective-permute-done((bf16[512,128]{1,0:T(8,128)(2,1)S(1)}, bf16[512,128]{1,0:T(8,128)(2,1)S(1)}, u32[]{:S(2)}, u32[]{:S(2)}) %collective-permute-start.1) | collective-permute-done | bytes 131104 | tf_op jit(solution)/shard_map/ppermute | solution.py:333
  43.1 1.1 %shard_map.80 = (bf16[512,512]{1,0:T(8,128)(2,1)S(1)}, bf16[512,512]{1,0:T(8,128)(2,1)S(1)}) custom-call(bf16[512,128]{1,0:T(8,128)(2,1)S(1)} %collective-permute-done.1.other_ref, bf16[512,256]{1,0:T(8,128)(2,1)S(1)} %get-tuple-element.44.q_ref, f32[512,512]{1,0:T(8,128)S(1)} %get-tuple-element.45.att_ref, f32[512,256]{1,0:T(8,128)S(1)} %get-tuple-element.47.kept_ref, ...), custom_call_target="tpu_custom_call" | custom-call | flops 1000000000 | bytes 3016704 | tf_op jit(solution)/shard_map/pallas_call | solution.py:33
  44.2 0.3 collective-permute-start.3
  44.5 1.5 %shard_map.82 = bf16[512,512]{1,0:T(8,128)(2,1)S(1)} custom-call(bf16[512,512]{1,0:T(8,128)(2,1)S(1)} %get-tuple-element.51.gated_ref, bf16[512,2048]{1,0:T(8,128)(2,1)} %w_hbm.5), custom_call_target="tpu_custom_call" | custom-call | flops 1000000000 | bytes 2621440 | tf_op jit(solution)/shard_map/pallas_call | solution.py:33
  46.0 1.9 %collective-permute-start.2 = (bf16[512,512]{1,0:T(8,128)(2,1)S(1)}, bf16[512,512]{1,0:T(8,128)(2,1)S(1)}, u32[]{:S(2)}, u32[]{:S(2)}) collective-permute-start(bf16[512,512]{1,0:T(8,128)(2,1)S(1)} %shard_map.82), channel_id=1, source_target_pairs={{1,0},{2,1},{3,2},{0,3},{7,4},{4,5},{5,6},{6,7},{9,8},{10,9},{11,1... | collective-permute-start | bytes 1572872 | tf_op jit(solution)/shard_map/ppermute | solution.py:357
  47.8 1.9 %shard_map.81 = (f32[512,512]{1,0:T(8,128)S(1)}, f32[512,512]{1,0:T(8,128)S(1)}) custom-call(bf16[512,512]{1,0:T(8,128)(2,1)S(1)} %get-tuple-element.51.gated_ref, bf16[512,2048]{1,0:T(8,128)(2,1)} %w_hbm.5), custom_call_target="tpu_custom_call" | custom-call | flops 1000000000 | bytes 2621440 | tf_op jit(solution)/shard_map/pallas_call | solution.py:33
  49.8 8.0 %collective-permute-done.3.far_ref = bf16[512,512]{1,0:T(8,128)(2,1)S(1)} collective-permute-done((bf16[512,512]{1,0:T(8,128)(2,1)S(1)}, bf16[512,512]{1,0:T(8,128)(2,1)S(1)}, u32[]{:S(2)}, u32[]{:S(2)}) %collective-permute-start.3) | collective-permute-done | bytes 524320 | tf_op jit(solution)/shard_map/ppermute | solution.py:354
  57.8 0.1 shard_map.83
  57.9 0.1 collective-permute-start.4
  58.0 1.4 %collective-permute-done.2.direct_ref = bf16[512,512]{1,0:T(8,128)(2,1)S(1)} collective-permute-done((bf16[512,512]{1,0:T(8,128)(2,1)S(1)}, bf16[512,512]{1,0:T(8,128)(2,1)S(1)}, u32[]{:S(2)}, u32[]{:S(2)}) %collective-permute-start.2) | collective-permute-done | bytes 524320 | tf_op jit(solution)/shard_map/ppermute | solution.py:357
  59.4 7.7 %collective-permute-done.4.passed_ref = bf16[512,512]{1,0:T(8,128)(2,1)S(1)} collective-permute-done((bf16[512,512]{1,0:T(8,128)(2,1)S(1)}, bf16[512,512]{1,0:T(8,128)(2,1)S(1)}, u32[]{:S(2)}, u32[]{:S(2)}) %collective-permute-start.4) | collective-permute-done | bytes 524320 | tf_op jit(solution)/shard_map/ppermute | solution.py:368
  67.2 0.9 %shard_map.84 = bf16[512,512]{1,0:T(8,128)(2,1)} custom-call(f32[512,512]{1,0:T(8,128)S(1)} %get-tuple-element.52.own_ref, bf16[512,512]{1,0:T(8,128)(2,1)S(1)} %collective-permute-done.2.direct_ref, bf16[512,512]{1,0:T(8,128)(2,1)S(1)} %collective-permute-done.4.passed_ref), custom_call_target="tpu_custom_call" | custom-call | flops 1000000000 | bytes 2097152 | tf_op jit(solution)/shard_map/pallas_call | solution.py:33
  (3 shorter events, 0.0 us)
Async XLA Ops:
  1.8 1.4 %collective-permute-start = (bf16[528,128]{1,0:T(8,128)(2,1)S(1)}, bf16[528,128]{1,0:T(8,128)(2,1)S(1)}, u32[]{:S(2)}, u32[]{:S(2)}) collective-permute-start(bf16[528,128]{1,0:T(8,128)(2,1)S(1)} %get-tuple-element.32), channel_id=1, source_target_pairs={{0,4},{4,0},{1,5},{5,1},{2,6},{6,2},{3,7},{7,3},{8,12},{12,8},{9,1... | collective-permute-start | bytes 405512 | tf_op jit(solution)/shard_map/ppermute | solution.py:299
  3.3 28.0 %copy-start = (f32[512]{0:T(512)S(1)}, f32[512]{0:T(512)}, u32[]{:S(2)}) copy-start(f32[512]{0:T(512)} %param.12) | copy-start | bytes 6148
  27.4 14.2 %all-to-all-start.1 = ((bf16[32,16,128]{2,1,0:T(8,128)(2,1)}), bf16[32,16,128]{2,1,0:T(8,128)(2,1)S(1)}, u32[]{:S(2)}, u32[]{:S(2)}) async-start(bf16[32,16,128]{2,1,0:T(8,128)(2,1)} %shard_map.76), calls=%async_computation.1 | async-start | bytes 262144 | tf_op jit(solution)/shard_map/all_to_all | solution.py:327
  41.7 1.4 %collective-permute-start.1 = (bf16[512,128]{1,0:T(8,128)(2,1)S(1)}, bf16[512,128]{1,0:T(8,128)(2,1)S(1)}, u32[]{:S(2)}, u32[]{:S(2)}) collective-permute-start(bf16[512,128]{1,0:T(8,128)(2,1)S(1)} %get-tuple-element.43), channel_id=1, source_target_pairs={{0,4},{4,0},{1,5},{5,1},{2,6},{6,2},{3,7},{7,3},{8,12},{12,8},{9,1... | collective-permute-start | bytes 393224 | tf_op jit(solution)/shard_map/ppermute | solution.py:333
  44.2 13.7 %collective-permute-start.3 = (bf16[512,512]{1,0:T(8,128)(2,1)S(1)}, bf16[512,512]{1,0:T(8,128)(2,1)S(1)}, u32[]{:S(2)}, u32[]{:S(2)}) collective-permute-start(bf16[512,512]{1,0:T(8,128)(2,1)S(1)} %get-tuple-element.54), channel_id=1, source_target_pairs={{0,1},{1,2},{2,3},{3,0},{4,7},{5,4},{6,5},{7,6},{8,9},{9,10},{10,1... | collective-permute-start | bytes 1572872 | tf_op jit(solution)/shard_map/ppermute | solution.py:354
  46.0 13.5 %collective-permute-start.2 = (bf16[512,512]{1,0:T(8,128)(2,1)S(1)}, bf16[512,512]{1,0:T(8,128)(2,1)S(1)}, u32[]{:S(2)}, u32[]{:S(2)}) collective-permute-start(bf16[512,512]{1,0:T(8,128)(2,1)S(1)} %shard_map.82), channel_id=1, source_target_pairs={{1,0},{2,1},{3,2},{0,3},{7,4},{4,5},{5,6},{6,7},{9,8},{10,9},{11,1... | collective-permute-start | bytes 1572872 | tf_op jit(solution)/shard_map/ppermute | solution.py:357
  57.9 9.3 %collective-permute-start.4 = (bf16[512,512]{1,0:T(8,128)(2,1)S(1)}, bf16[512,512]{1,0:T(8,128)(2,1)S(1)}, u32[]{:S(2)}, u32[]{:S(2)}) collective-permute-start(bf16[512,512]{1,0:T(8,128)(2,1)S(1)} %shard_map.83), channel_id=1, source_target_pairs={{0,1},{1,2},{2,3},{3,0},{4,7},{5,4},{6,5},{7,6},{8,9},{9,10},{10,1... | collective-permute-start | bytes 1572872 | tf_op jit(solution)/shard_map/ppermute | solution.py:368

commit v3 on v0

--- a/solution.py
+++ b/solution.py
@@ -90,9 +90,9 @@
     after = dot(mask, gate)
     total = after[0:1] + gate[0:1].astype(F32)
     k_copy.wait()
+    v_copy.wait()
     k_state = (k_ref[...].astype(F32) * jnp.exp(after)).astype(BF16)
     state_ref[...] = k_state
-    v_copy.wait()
     theirs = columns(1 - lax.axis_index("core"), half)
     state = dot(v_ref[:, theirs], k_state, ((0,), (0,))).astype(BF16)
     swap_ref[0:half, :] = state[:, :LANE]
@@ -142,15 +142,30 @@
     out_ref[:, 2 * rows :, :] = jnp.broadcast_to(tail[None], (pieces, 8, LANE)).astype(BF16)
 
 
-def scan_body(in_ref, out_ref):
+CHUNKS = 4
+
+
+def flush(copies, sems, src, dst, index):
+    size = src.shape[0] // CHUNKS
+    at = pl.ds(index * size, size)
+    copies.append(pltpu.make_async_copy(src.at[at], dst.at[at], sems.at[index]))
+    copies[-1].start()
+
+
+def scan_body(in_ref, out_hbm, out_ref, sems):
     pieces, rows = (in_ref.shape[0], out_ref.shape[1] // 2)
     left = right = jnp.zeros((rows, LANE), F32)
+    copies = []
     for j in range(pieces):
         out_ref[j, 0:rows, :] = left.astype(BF16)
         out_ref[j, rows : 2 * rows, :] = right.astype(BF16)
         tail = in_ref[j, 2 * rows :, :].astype(F32)
         left = left * jnp.exp(tail[0:1] + tail[2:3]) + in_ref[j, 0:rows, :].astype(F32)
         right = right * jnp.exp(tail[1:2] + tail[3:4]) + in_ref[j, rows : 2 * rows, :].astype(F32)
+        if (j + 1) % (pieces // CHUNKS) == 0:
+            flush(copies, sems, out_ref, out_hbm, j * CHUNKS // pieces)
+    for copy in copies:
+        copy.wait()
 
 
 def part_body(in_ref, first_ref, decay_ref, keep_ref, send_ref):
@@ -228,7 +243,7 @@
 
 def finish_body(
     other_ref, q_ref, att_ref, kept_ref, square_ref, scale_ref, w_ref,
-    gated_ref, far_up_ref, far_down_ref,
+    gated_ref, far_on_ref, far_back_ref,
 ):
     half = other_ref.shape[0] // 2
     core = lax.axis_index("core")
@@ -240,9 +255,9 @@
     inverse = lax.rsqrt(total * (1.0 / DV) + 1e-05)
     gated_ref[:, there] = (attention * inverse * scale_ref[:, there].astype(F32)).astype(BF16)
     gated_ref[:, here] = (kept_ref[...] * inverse * scale_ref[:, here].astype(F32)).astype(BF16)
-    split = far_up_ref.shape[0]
-    far_up_ref[...] = dot(gated_ref[:split, :], w_ref[...]).astype(BF16)
-    far_down_ref[...] = dot(gated_ref[split:, :], w_ref[...]).astype(BF16)
+    rows = far_on_ref.shape[0]
+    far_on_ref[...] = dot(gated_ref[:rows, :], w_ref[...]).astype(BF16)
+    far_back_ref[...] = dot(gated_ref[rows:, :], w_ref[...]).astype(BF16)
 
 
 def fetch_columns(w_hbm, w_ref, sems, *shifts):
@@ -251,39 +266,48 @@
     return fetch(sems, *pairs)
 
 
-def direct_body(gated_ref, w_hbm, up_ref, down_ref, w_ref, sems):
-    copies = fetch_columns(w_hbm, w_ref, sems, 1, 3)
-    length, split = (gated_ref.shape[0], down_ref.shape[0])
+def onward():
+    return jnp.where(lax.axis_index("core") == 0, 1, lax.axis_size("head") - 1)
+
+
+def direct_body(gated_ref, w_hbm, on_ref, back_ref, w_ref, sems):
+    copies = fetch_columns(w_hbm, w_ref, sems, onward(), lax.axis_size("head") - onward())
+    half = on_ref.shape[0]
     copies[0].wait()
-    up_ref[...] = dot(gated_ref[length - up_ref.shape[0] :, :], w_ref[0]).astype(BF16)
+    on_ref[...] = dot(gated_ref[half:, :], w_ref[0]).astype(BF16)
     copies[1].wait()
-    down_ref[...] = dot(gated_ref[:split, :], w_ref[1]).astype(BF16)
-
-
-def near_body(gated_ref, w_hbm, up_ref, down_ref, own_ref, w_ref, sems):
-    copies = fetch_columns(w_hbm, w_ref, sems, 1, 3, 0)
-    split = up_ref.shape[0]
+    back_ref[...] = dot(gated_ref[:half, :], w_ref[1]).astype(BF16)
+
+
+def near_body(gated_ref, w_hbm, on_ref, back_ref, own_ref, w_ref, sems):
+    copies = fetch_columns(w_hbm, w_ref, sems, onward(), lax.axis_size("head") - onward(), 0)
+    half = on_ref.shape[0]
     copies[0].wait()
-    up_ref[...] = dot(gated_ref[:split, :], w_ref[0])
+    on_ref[...] = dot(gated_ref[:half, :], w_ref[0])
     copies[1].wait()
-    down_ref[...] = dot(gated_ref[split:, :], w_ref[1])
+    back_ref[...] = dot(gated_ref[half:, :], w_ref[1])
     copies[2].wait()
     own_ref[...] = dot(gated_ref[...], w_ref[2])
 
 
-def pass_body(up_ref, down_ref, far_up_ref, far_down_ref, up_out_ref, down_out_ref):
-    up_out_ref[...] = (up_ref[...] + far_up_ref[...].astype(F32)).astype(BF16)
-    down_out_ref[...] = (down_ref[...] + far_down_ref[...].astype(F32)).astype(BF16)
-
-
-def sum_body(own_ref, below_a_ref, below_b_ref, above_a_ref, above_b_ref, out_ref):
-    split = below_a_ref.shape[0]
-    for at, below, above in (
-        (slice(0, split), below_a_ref, above_a_ref),
-        (slice(split, own_ref.shape[0]), below_b_ref, above_b_ref),
-    ):
-        total = own_ref[at, :] + below[...].astype(F32) + above[...].astype(F32)
+def pass_body(on_ref, back_ref, far_on_ref, far_back_ref, on_out_ref, back_out_ref):
+    on_out_ref[...] = (on_ref[...] + far_on_ref[...].astype(F32)).astype(BF16)
+    back_out_ref[...] = (back_ref[...] + far_back_ref[...].astype(F32)).astype(BF16)
+
+
+def sum_body(own_ref, on_a_ref, on_b_ref, back_a_ref, back_b_ref, out_hbm, out_ref, sems):
+    length, half = (own_ref.shape[0], on_a_ref.shape[0])
+    size = length // CHUNKS
+    copies = []
+    for i in range(CHUNKS):
+        at, start = slice(i * size, (i + 1) * size), i * size % half
+        part = slice(start, start + size)
+        on, back = (on_a_ref, back_a_ref) if i * size < half else (on_b_ref, back_b_ref)
+        total = own_ref[at, :] + on[part, :].astype(F32) + back[part, :].astype(F32)
         out_ref[at, :] = total.astype(BF16)
+        flush(copies, sems, out_ref, out_hbm, i)
+    for copy in copies:
+        copy.wait()
 
 
 def ring(axis, shift):
@@ -317,7 +341,15 @@
         swapped,
     )
     slices = lax.all_to_all(sent, CHIPS, 0, 0, tiled=True)
-    prefixes = call(scan_body, shape((pieces, 2 * rows, LANE), BF16), slices)
+    carried = shape((pieces, 2 * rows, LANE), BF16)
+    prefixes = call(
+        scan_body,
+        carried,
+        slices,
+        scratch=[pltpu.VMEM(carried.shape, BF16)],
+        copies=CHUNKS,
+        outs_in=HBM,
+    )
     prefixes, queries = lax.optimization_barrier((prefixes, queries))
     inputs = (queries, key_vectors, values, log_gate, out_gate)
     att_local, q_start, scale, w_far = call(
@@ -345,11 +377,11 @@
     kept, square = call(
         keep_body, (shape((length, half), F32), shape((length, 1), F32)), keep, q_start, att_local
     )
-    split = length // 2
-    first, last = shape((split, width), BF16), shape((length - split, width), BF16)
-    gated, far_up, far_down = call(
+    near = shape((length // 2, width), BF16)
+    near_f = shape((length // 2, width), F32)
+    gated, far_on, far_back = call(
         finish_body,
-        (shape((length, DV), BF16), first, last),
+        (shape((length, DV), BF16), near, near),
         other,
         q_start,
         att_local,
@@ -358,34 +390,46 @@
         scale,
         w_far,
     )
-    up, down = ring("head", 1), ring("head", -1)
-    far_up = lax.ppermute(far_up, "head", up)
-    far_down = lax.ppermute(far_down, "head", down)
-    up_b, down_a = call(
+    heads = lax.axis_size("head")
+    on = [(c * heads + y, c * heads + (y + 1 - 2 * c) % heads) for c in (0, 1) for y in range(heads)]
+    back = [(target, source) for source, target in on]
+    group = ("core", "head")
+    far_on = lax.ppermute(far_on, group, on)
+    far_back = lax.ppermute(far_back, group, back)
+    on_b, back_a = call(
         direct_body,
-        (last, first),
+        (near, near),
         gated,
         out_weight,
         fetched=(1,),
         scratch=[pltpu.VMEM((2, DV, width), BF16)],
         copies=2,
     )
-    below_b = lax.ppermute(up_b, "head", up)
-    above_a = lax.ppermute(down_a, "head", down)
-    up_a, down_b, own_part = call(
+    on_b = lax.ppermute(on_b, group, on)
+    back_a = lax.ppermute(back_a, group, back)
+    on_a, back_b, own_part = call(
         near_body,
-        (shape(first.shape, F32), shape(last.shape, F32), shape((length, width), F32)),
+        (near_f, near_f, shape((length, width), F32)),
         gated,
         out_weight,
         fetched=(1,),
         scratch=[pltpu.VMEM((3, DV, width), BF16)],
         copies=3,
     )
-    up_a, down_b = call(pass_body, (first, last), up_a, down_b, far_up, far_down)
-    below_a = lax.ppermute(up_a, "head", up)
-    above_b = lax.ppermute(down_b, "head", down)
+    on_a, back_b = call(pass_body, (near, near), on_a, back_b, far_on, far_back)
+    on_a = lax.ppermute(on_a, group, on)
+    back_b = lax.ppermute(back_b, group, back)
     return call(
-        sum_body, shape((length, width), BF16), own_part, below_a, below_b, above_a, above_b
+        sum_body,
+        shape((length, width), BF16),
+        own_part,
+        on_a,
+        on_b,
+        back_a,
+        back_b,
+        scratch=[pltpu.VMEM((length, width), BF16)],
+        copies=CHUNKS,
+        outs_in=HBM,
     )
 
 

time: 66.8 us -> 67.9 us (1.016)
  the two profiles are of different devices: /device:TPU:24 before, /device:TPU:1 now
where the time goes in v3:
time: 67.9 us; the launch traced here: 67.6 us
  blocking collectives  18.8 us (28%)
  starting transfers between devices  18.4 us (27%)
  waiting for transfers between devices  15.3 us (23%)
  Pallas kernels  15 us (22%)
    all_to_all x1, blocking collectives, shards(): slices = lax.all_to_all(sent, CHIPS, 0, 0, tiled=True)  18.8 us
    pallas_call x12, Pallas kernels, call(): pl.pallas_call(body, out_shape=outs, in_specs=[HBM if i in fetched else V...  15 us
    all_to_all x1, starting transfers between devices, shards(): entering = lax.all_to_all(prefixes, CHIPS, 0, 0, tiled=True)  5.65 us
    all_to_all x1, waiting for transfers between devices, shards(): entering = lax.all_to_all(prefixes, CHIPS, 0, 0, tiled=True)  4.31 us
    ppermute x1, starting transfers between devices, shards(): swapped = lax.ppermute(swap, 'core', ring('core', 1))  3.3 us
    ppermute x1, waiting for transfers between devices, shards(): back_a = lax.ppermute(back_a, group, back)  3.22 us
    ppermute x1, starting transfers between devices, shards(): far_on = lax.ppermute(far_on, group, on)  2.81 us
    ppermute x1, starting transfers between devices, shards(): on_b = lax.ppermute(on_b, group, on)  2.75 us
  transfers between devices with their start and end apart: 9, of which 7 were waited for; matrix products, arithmetic and copies ran while one was open for 0% of the time, Pallas kernels for 15%

profile of v3, /device:TPU:1, one launch (start us, length us, event | category | flops | bytes accessed | tf_op | source)
XLA Modules:
  0.0 67.6 jit_solution(1326489988509687892)
XLA Ops:
  0.0 1.7 %shard_map.73 = (bf16[528,128]{1,0:T(8,128)(2,1)S(1)}, f32[8,128]{1,0:T(8,128)S(1)}, bf16[512,256]{1,0:T(8,128)(2,1)S(1)}) custom-call(bf16[512,256]{1,0:T(8,128)(2,1)} %k_hbm.3, bf16[512,512]{1,0:T(8,128)(2,1)} %v_hbm.5, bf16[512,256]{1,0:T(8,128)(2,1)} %g_hbm.3), custom_call_target="tpu_custom_call" | custom-call | flops 1000000000 | bytes 1048576 | tf_op jit(solution)/shard_map/pallas_call | solution.py:33
  1.7 3.3 %collective-permute-start = (bf16[528,128]{1,0:T(8,128)(2,1)S(1)}, bf16[528,128]{1,0:T(8,128)(2,1)S(1)}, u32[]{:S(2)}, u32[]{:S(2)}) collective-permute-start(bf16[528,128]{1,0:T(8,128)(2,1)S(1)} %get-tuple-element.38), channel_id=1, source_target_pairs={{0,4},{4,0},{1,5},{5,1},{2,6},{6,2},{3,7},{7,3},{8,12},{12,8},{9,1... | collective-permute-start | bytes 405512 | tf_op jit(solution)/shard_map/ppermute | solution.py:334
  5.0 1.3 %shard_map.74.own_ref = f32[512,128]{1,0:T(8,128)S(1)} custom-call(bf16[512,512]{1,0:T(8,128)(2,1)} %v_hbm.5, bf16[512,256]{1,0:T(8,128)(2,1)S(1)} %get-tuple-element.36.state_ref), custom_call_target="tpu_custom_call" | custom-call | flops 1000000000 | bytes 786432 | tf_op jit(solution)/shard_map/pallas_call | solution.py:33
  6.4 18.8 %all_to_all.10.in_ref = bf16[32,24,128]{2,1,0:T(8,128)(2,1)S(1)} all-to-all(bf16[32,24,128]{2,1,0:T(8,128)(2,1)S(1)} %get-tuple-element.39), channel_id=1, replica_groups=mesh['chip_x'=4,'chip_z'=8,'core'=2,'head'=4] {'chip_x','chip_z'}, dimensions={0} | all-to-all | bytes 393216 | tf_op jit(solution)/shard_map/all_to_all | solution.py:343
  25.2 0.7 %shard_map.76 = bf16[32,16,128]{2,1,0:T(8,128)(2,1)} custom-call(bf16[32,24,128]{2,1,0:T(8,128)(2,1)S(1)} %all_to_all.10.in_ref), custom_call_target="tpu_custom_call" | custom-call | flops 1000000000 | bytes 196608 | tf_op jit(solution)/shard_map/pallas_call | solution.py:33
  25.9 5.7 %all-to-all-start.1 = ((bf16[32,16,128]{2,1,0:T(8,128)(2,1)}), bf16[32,16,128]{2,1,0:T(8,128)(2,1)S(1)}, u32[]{:S(2)}, u32[]{:S(2)}) async-start(bf16[32,16,128]{2,1,0:T(8,128)(2,1)} %shard_map.76), calls=%async_computation.1 | async-start | bytes 262144 | tf_op jit(solution)/shard_map/all_to_all | solution.py:370
  31.6 4.8 %shard_map.77 = (f32[512,512]{1,0:T(8,128)S(1)}, bf16[512,256]{1,0:T(8,128)(2,1)S(1)}, bf16[512,512]{1,0:T(8,128)(2,1)S(1)}, bf16[512,512]{1,0:T(8,128)(2,1)S(1)}) custom-call(bf16[512,256]{1,0:T(8,128)(2,1)} %q_hbm, bf16[512,256]{1,0:T(8,128)(2,1)} %k_hbm.3, bf16[512,512]{1,0:T(8,128)(2,1)} %v_hbm.5, bf16[512,256]{1,0:T(8,128)(2,1)} %g_hbm.3, ...), custom_call_target="tpu_custom_call" | custom-call | flops 1000000000 | bytes 3934208 | tf_op jit(solution)/shard_map/pallas_call | solution.py:33
  36.4 4.3 %all-to-all-done.1.in_ref = bf16[32,16,128]{2,1,0:T(8,128)(2,1)S(1)} async-done(((bf16[32,16,128]{2,1,0:T(8,128)(2,1)}), bf16[32,16,128]{2,1,0:T(8,128)(2,1)S(1)}, u32[]{:S(2)}, u32[]{:S(2)}) %all-to-all-start.1) | async-done | bytes 131104 | tf_op jit(solution)/shard_map/all_to_all | solution.py:370
  40.8 2.3 %collective-permute-start.1 = (bf16[512,128]{1,0:T(8,128)(2,1)S(1)}, bf16[512,128]{1,0:T(8,128)(2,1)S(1)}, u32[]{:S(2)}, u32[]{:S(2)}) collective-permute-start(bf16[512,128]{1,0:T(8,128)(2,1)S(1)} %get-tuple-element.49), channel_id=1, source_target_pairs={{0,4},{4,0},{1,5},{5,1},{2,6},{6,2},{3,7},{7,3},{8,12},{12,8},{9,1... | collective-permute-start | bytes 393224 | tf_op jit(solution)/shard_map/ppermute | solution.py:376
  43.2 0.4 shard_map.79
  43.5 0.6 collective-permute-done.1.other_ref
  44.1 1.2 %shard_map.80 = (bf16[512,512]{1,0:T(8,128)(2,1)S(1)}, bf16[256,512]{1,0:T(8,128)(2,1)S(1)}, bf16[256,512]{1,0:T(8,128)(2,1)S(1)}) custom-call(bf16[512,128]{1,0:T(8,128)(2,1)S(1)} %collective-permute-done.1.other_ref, bf16[512,256]{1,0:T(8,128)(2,1)S(1)} %get-tuple-element.50.q_ref, f32[512,512]{1,0:T(8,128)S(1)} %get-tuple-element.51.att_ref, ...), custom_call_target="tpu_custom_call" | custom-call | flops 1000000000 | bytes 3016704 | tf_op jit(solution)/shard_map/pallas_call | solution.py:33
  45.3 2.8 %collective-permute-start.2 = (bf16[256,512]{1,0:T(8,128)(2,1)S(1)}, bf16[256,512]{1,0:T(8,128)(2,1)S(1)}, u32[]{:S(2)}, u32[]{:S(2)}) collective-permute-start(bf16[256,512]{1,0:T(8,128)(2,1)S(1)} %get-tuple-element.61), channel_id=1, source_target_pairs={{0,1},{1,2},{2,3},{3,0},{4,7},{5,4},{6,5},{7,6},{8,9},{9,10},{10,1... | collective-permute-start | bytes 786440 | tf_op jit(solution)/shard_map/ppermute | solution.py:397
  48.2 1.7 %shard_map.83 = (bf16[256,512]{1,0:T(8,128)(2,1)S(1)}, bf16[256,512]{1,0:T(8,128)(2,1)S(1)}) custom-call(bf16[512,512]{1,0:T(8,128)(2,1)S(1)} %get-tuple-element.57.gated_ref, bf16[512,2048]{1,0:T(8,128)(2,1)} %w_hbm.5), custom_call_target="tpu_custom_call" | custom-call | flops 1000000000 | bytes 2621440 | tf_op jit(solution)/shard_map/pallas_call | solution.py:33
  49.8 2.7 %collective-permute-start.5 = (bf16[256,512]{1,0:T(8,128)(2,1)S(1)}, bf16[256,512]{1,0:T(8,128)(2,1)S(1)}, u32[]{:S(2)}, u32[]{:S(2)}) collective-permute-start(bf16[256,512]{1,0:T(8,128)(2,1)S(1)} %get-tuple-element.64), channel_id=1, source_target_pairs={{0,1},{1,2},{2,3},{3,0},{4,7},{5,4},{6,5},{7,6},{8,9},{9,10},{10,1... | collective-permute-start | bytes 786440 | tf_op jit(solution)/shard_map/ppermute | solution.py:408
  52.6 2.1 %shard_map.81 = (f32[256,512]{1,0:T(8,128)S(1)}, f32[256,512]{1,0:T(8,128)S(1)}, f32[512,512]{1,0:T(8,128)S(1)}) custom-call(bf16[512,512]{1,0:T(8,128)(2,1)S(1)} %get-tuple-element.57.gated_ref, bf16[512,2048]{1,0:T(8,128)(2,1)} %w_hbm.5), custom_call_target="tpu_custom_call" | custom-call | flops 1000000000 | bytes 2621440 | tf_op jit(solution)/shard_map/pallas_call | solution.py:33
  54.7 1.7 %collective-permute-done.3.far_back_ref = bf16[256,512]{1,0:T(8,128)(2,1)S(1)} collective-permute-done((bf16[256,512]{1,0:T(8,128)(2,1)S(1)}, bf16[256,512]{1,0:T(8,128)(2,1)S(1)}, u32[]{:S(2)}, u32[]{:S(2)}) %collective-permute-start.3) | collective-permute-done | bytes 262176 | tf_op jit(solution)/shard_map/ppermute | solution.py:398
  56.5 1.1 %collective-permute-start.4 = (bf16[256,512]{1,0:T(8,128)(2,1)S(1)}, bf16[256,512]{1,0:T(8,128)(2,1)S(1)}, u32[]{:S(2)}, u32[]{:S(2)}) collective-permute-start(bf16[256,512]{1,0:T(8,128)(2,1)S(1)} %get-tuple-element.63), channel_id=1, source_target_pairs={{0,1},{1,2},{2,3},{3,0},{4,7},{5,4},{6,5},{7,6},{8,9},{9,10},{10,1... | collective-permute-start | bytes 786440 | tf_op jit(solution)/shard_map/ppermute | solution.py:420
  57.6 0.5 collective-permute-start.7
  58.0 0.8 %collective-permute-done.5.on_b_ref = bf16[256,512]{1,0:T(8,128)(2,1)S(1)} collective-permute-done((bf16[256,512]{1,0:T(8,128)(2,1)S(1)}, bf16[256,512]{1,0:T(8,128)(2,1)S(1)}, u32[]{:S(2)}, u32[]{:S(2)}) %collective-permute-start.5) | collective-permute-done | bytes 262176 | tf_op jit(solution)/shard_map/ppermute | solution.py:408
  58.8 3.2 %collective-permute-done.6.back_a_ref = bf16[256,512]{1,0:T(8,128)(2,1)S(1)} collective-permute-done((bf16[256,512]{1,0:T(8,128)(2,1)S(1)}, bf16[256,512]{1,0:T(8,128)(2,1)S(1)}, u32[]{:S(2)}, u32[]{:S(2)}) %collective-permute-start.6) | collective-permute-done | bytes 262176 | tf_op jit(solution)/shard_map/ppermute | solution.py:409
  62.1 2.4 %collective-permute-done.4.on_a_ref = bf16[256,512]{1,0:T(8,128)(2,1)S(1)} collective-permute-done((bf16[256,512]{1,0:T(8,128)(2,1)S(1)}, bf16[256,512]{1,0:T(8,128)(2,1)S(1)}, u32[]{:S(2)}, u32[]{:S(2)}) %collective-permute-start.4) | collective-permute-done | bytes 262176 | tf_op jit(solution)/shard_map/ppermute | solution.py:420
  64.5 2.3 %collective-permute-done.7.back_b_ref = bf16[256,512]{1,0:T(8,128)(2,1)S(1)} collective-permute-done((bf16[256,512]{1,0:T(8,128)(2,1)S(1)}, bf16[256,512]{1,0:T(8,128)(2,1)S(1)}, u32[]{:S(2)}, u32[]{:S(2)}) %collective-permute-start.7) | collective-permute-done | bytes 262176 | tf_op jit(solution)/shard_map/ppermute | solution.py:421
  66.7 0.9 %shard_map.84 = bf16[512,512]{1,0:T(8,128)(2,1)} custom-call(f32[512,512]{1,0:T(8,128)S(1)} %get-tuple-element.58.own_ref, bf16[256,512]{1,0:T(8,128)(2,1)S(1)} %collective-permute-done.4.on_a_ref, bf16[256,512]{1,0:T(8,128)(2,1)S(1)} %collective-permute-done.5.on_b_ref, bf16[256,512]{1,0:T(8,128)(2,1)S(1)} %collective-permute-done.6.back_a_ref, ...), custom_call_target="tpu_custom_call" | custom-call | flops 1000000000 | bytes 2097152 | tf_op jit(solution)/shard_map/pallas_call | solution.py:33
  (9 shorter events, 0.3 us)
Async XLA Ops:
  1.7 4.6 %collective-permute-start = (bf16[528,128]{1,0:T(8,128)(2,1)S(1)}, bf16[528,128]{1,0:T(8,128)(2,1)S(1)}, u32[]{:S(2)}, u32[]{:S(2)}) collective-permute-start(bf16[528,128]{1,0:T(8,128)(2,1)S(1)} %get-tuple-element.38), channel_id=1, source_target_pairs={{0,4},{4,0},{1,5},{5,1},{2,6},{6,2},{3,7},{7,3},{8,12},{12,8},{9,1... | collective-permute-start | bytes 405512 | tf_op jit(solution)/shard_map/ppermute | solution.py:334
  6.4 25.2 %copy-start = (f32[512]{0:T(512)S(1)}, f32[512]{0:T(512)}, u32[]{:S(2)}) copy-start(f32[512]{0:T(512)} %param.12) | copy-start | bytes 6148
  25.9 14.8 %all-to-all-start.1 = ((bf16[32,16,128]{2,1,0:T(8,128)(2,1)}), bf16[32,16,128]{2,1,0:T(8,128)(2,1)S(1)}, u32[]{:S(2)}, u32[]{:S(2)}) async-start(bf16[32,16,128]{2,1,0:T(8,128)(2,1)} %shard_map.76), calls=%async_computation.1 | async-start | bytes 262144 | tf_op jit(solution)/shard_map/all_to_all | solution.py:370
  40.8 3.3 %collective-permute-start.1 = (bf16[512,128]{1,0:T(8,128)(2,1)S(1)}, bf16[512,128]{1,0:T(8,128)(2,1)S(1)}, u32[]{:S(2)}, u32[]{:S(2)}) collective-permute-start(bf16[512,128]{1,0:T(8,128)(2,1)S(1)} %get-tuple-element.49), channel_id=1, source_target_pairs={{0,4},{4,0},{1,5},{5,1},{2,6},{6,2},{3,7},{7,3},{8,12},{12,8},{9,1... | collective-permute-start | bytes 393224 | tf_op jit(solution)/shard_map/ppermute | solution.py:376
  45.3 9.4 %collective-permute-start.2 = (bf16[256,512]{1,0:T(8,128)(2,1)S(1)}, bf16[256,512]{1,0:T(8,128)(2,1)S(1)}, u32[]{:S(2)}, u32[]{:S(2)}) collective-permute-start(bf16[256,512]{1,0:T(8,128)(2,1)S(1)} %get-tuple-element.61), channel_id=1, source_target_pairs={{0,1},{1,2},{2,3},{3,0},{4,7},{5,4},{6,5},{7,6},{8,9},{9,10},{10,1... | collective-permute-start | bytes 786440 | tf_op jit(solution)/shard_map/ppermute | solution.py:397
  48.2 8.3 %collective-permute-start.3 = (bf16[256,512]{1,0:T(8,128)(2,1)S(1)}, bf16[256,512]{1,0:T(8,128)(2,1)S(1)}, u32[]{:S(2)}, u32[]{:S(2)}) collective-permute-start(bf16[256,512]{1,0:T(8,128)(2,1)S(1)} %get-tuple-element.62), channel_id=1, source_target_pairs={{1,0},{2,1},{3,2},{0,3},{7,4},{4,5},{5,6},{6,7},{9,8},{10,9},{11,1... | collective-permute-start | bytes 786440 | tf_op jit(solution)/shard_map/ppermute | solution.py:398
  49.8 9.0 %collective-permute-start.5 = (bf16[256,512]{1,0:T(8,128)(2,1)S(1)}, bf16[256,512]{1,0:T(8,128)(2,1)S(1)}, u32[]{:S(2)}, u32[]{:S(2)}) collective-permute-start(bf16[256,512]{1,0:T(8,128)(2,1)S(1)} %get-tuple-element.64), channel_id=1, source_target_pairs={{0,1},{1,2},{2,3},{3,0},{4,7},{5,4},{6,5},{7,6},{8,9},{9,10},{10,1... | collective-permute-start | bytes 786440 | tf_op jit(solution)/shard_map/ppermute | solution.py:408
  52.6 9.5 %collective-permute-start.6 = (bf16[256,512]{1,0:T(8,128)(2,1)S(1)}, bf16[256,512]{1,0:T(8,128)(2,1)S(1)}, u32[]{:S(2)}, u32[]{:S(2)}) collective-permute-start(bf16[256,512]{1,0:T(8,128)(2,1)S(1)} %get-tuple-element.65), channel_id=1, source_target_pairs={{1,0},{2,1},{3,2},{0,3},{7,4},{4,5},{5,6},{6,7},{9,8},{10,9},{11,1... | collective-permute-start | bytes 786440 | tf_op jit(solution)/shard_map/ppermute | solution.py:409
  56.5 8.0 %collective-permute-start.4 = (bf16[256,512]{1,0:T(8,128)(2,1)S(1)}, bf16[256,512]{1,0:T(8,128)(2,1)S(1)}, u32[]{:S(2)}, u32[]{:S(2)}) collective-permute-start(bf16[256,512]{1,0:T(8,128)(2,1)S(1)} %get-tuple-element.63), channel_id=1, source_target_pairs={{0,1},{1,2},{2,3},{3,0},{4,7},{5,4},{6,5},{7,6},{8,9},{9,10},{10,1... | collective-permute-start | bytes 786440 | tf_op jit(solution)/shard_map/ppermute | solution.py:420
  57.6 9.2 %collective-permute-start.7 = (bf16[256,512]{1,0:T(8,128)(2,1)S(1)}, bf16[256,512]{1,0:T(8,128)(2,1)S(1)}, u32[]{:S(2)}, u32[]{:S(2)}) collective-permute-start(bf16[256,512]{1,0:T(8,128)(2,1)S(1)} %get-tuple-element.66), channel_id=1, source_target_pairs={{1,0},{2,1},{3,2},{0,3},{7,4},{4,5},{5,6},{6,7},{9,8},{10,9},{11,1... | collective-permute-start | bytes 786440 | tf_op jit(solution)/shard_map/ppermute | solution.py:421

commit v4 on v0

--- a/solution.py
+++ b/solution.py
@@ -90,9 +90,9 @@
     after = dot(mask, gate)
     total = after[0:1] + gate[0:1].astype(F32)
     k_copy.wait()
+    v_copy.wait()
     k_state = (k_ref[...].astype(F32) * jnp.exp(after)).astype(BF16)
     state_ref[...] = k_state
-    v_copy.wait()
     theirs = columns(1 - lax.axis_index("core"), half)
     state = dot(v_ref[:, theirs], k_state, ((0,), (0,))).astype(BF16)
     swap_ref[0:half, :] = state[:, :LANE]
@@ -217,18 +217,23 @@
     far_copy.wait()
 
 
-def keep_body(keep_ref, q_ref, att_ref, out_ref, square_ref):
+def keep_body(
+    keep_ref, q_ref, att_ref, scale_ref, w_ref, gated_ref, square_ref, far_ref
+):
     half = keep_ref.shape[0] // 2
-    attention = att_ref[:, columns(lax.axis_index("core"), half)]
+    here = columns(lax.axis_index("core"), half)
+    attention = att_ref[:, here]
     attention = attention + dot(q_ref[:, :LANE], keep_ref[:half, :], ((1,), (1,)))
     attention = attention + dot(q_ref[:, LANE:], keep_ref[half:, :], ((1,), (1,)))
-    out_ref[...] = attention
+    gated = (attention * scale_ref[:, here].astype(F32)).astype(BF16)
+    gated_ref[...] = gated
+    far_ref[...] = dot(gated, w_ref[here, :])
     square_ref[...] = jnp.sum(attention * attention, axis=-1, keepdims=True)
 
 
 def finish_body(
-    other_ref, q_ref, att_ref, kept_ref, square_ref, scale_ref, w_ref,
-    gated_ref, far_up_ref, far_down_ref,
+    other_ref, q_ref, att_ref, kept_ref, square_ref, kept_far_ref, scale_ref, w_ref,
+    gated_ref, norm_ref, far_up_ref, far_down_ref,
 ):
     half = other_ref.shape[0] // 2
     core = lax.axis_index("core")
@@ -236,13 +241,17 @@
     attention = att_ref[:, there]
     attention = attention + dot(q_ref[:, :LANE], other_ref[:half, :], ((1,), (1,)))
     attention = attention + dot(q_ref[:, LANE:], other_ref[half:, :], ((1,), (1,)))
+    gated = (attention * scale_ref[:, there].astype(F32)).astype(BF16)
+    far = kept_far_ref[...] + dot(gated, w_ref[there, :])
     total = square_ref[...] + jnp.sum(attention * attention, axis=-1, keepdims=True)
-    inverse = lax.rsqrt(total * (1.0 / DV) + 1e-05)
-    gated_ref[:, there] = (attention * inverse * scale_ref[:, there].astype(F32)).astype(BF16)
-    gated_ref[:, here] = (kept_ref[...] * inverse * scale_ref[:, here].astype(F32)).astype(BF16)
+    norm = lax.rsqrt(total * (1.0 / DV) + 1e-05)
+    norm_ref[...] = norm
+    far = (far * norm).astype(BF16)
     split = far_up_ref.shape[0]
-    far_up_ref[...] = dot(gated_ref[:split, :], w_ref[...]).astype(BF16)
-    far_down_ref[...] = dot(gated_ref[split:, :], w_ref[...]).astype(BF16)
+    far_up_ref[...] = far[:split]
+    far_down_ref[...] = far[split:]
+    gated_ref[:, there] = gated
+    gated_ref[:, here] = kept_ref[...]
 
 
 def fetch_columns(w_hbm, w_ref, sems, *shifts):
@@ -251,24 +260,26 @@
     return fetch(sems, *pairs)
 
 
-def direct_body(gated_ref, w_hbm, up_ref, down_ref, w_ref, sems):
+def direct_body(gated_ref, norm_ref, w_hbm, up_ref, down_ref, w_ref, sems):
     copies = fetch_columns(w_hbm, w_ref, sems, 1, 3)
-    length, split = (gated_ref.shape[0], down_ref.shape[0])
+    half = up_ref.shape[0]
+    top, low = slice(0, half), slice(half, 2 * half)
     copies[0].wait()
-    up_ref[...] = dot(gated_ref[length - up_ref.shape[0] :, :], w_ref[0]).astype(BF16)
+    up_ref[...] = (dot(gated_ref[low, :], w_ref[0]) * norm_ref[low, :]).astype(BF16)
     copies[1].wait()
-    down_ref[...] = dot(gated_ref[:split, :], w_ref[1]).astype(BF16)
-
-
-def near_body(gated_ref, w_hbm, up_ref, down_ref, own_ref, w_ref, sems):
+    down_ref[...] = (dot(gated_ref[top, :], w_ref[1]) * norm_ref[top, :]).astype(BF16)
+
+
+def near_body(gated_ref, norm_ref, w_hbm, up_ref, down_ref, own_ref, w_ref, sems):
     copies = fetch_columns(w_hbm, w_ref, sems, 1, 3, 0)
-    split = up_ref.shape[0]
+    half = up_ref.shape[0]
+    top, low = slice(0, half), slice(half, 2 * half)
     copies[0].wait()
-    up_ref[...] = dot(gated_ref[:split, :], w_ref[0])
+    up_ref[...] = dot(gated_ref[top, :], w_ref[0]) * norm_ref[top, :]
     copies[1].wait()
-    down_ref[...] = dot(gated_ref[split:, :], w_ref[1])
+    down_ref[...] = dot(gated_ref[low, :], w_ref[1]) * norm_ref[low, :]
     copies[2].wait()
-    own_ref[...] = dot(gated_ref[...], w_ref[2])
+    own_ref[...] = dot(gated_ref[...], w_ref[2]) * norm_ref[...]
 
 
 def pass_body(up_ref, down_ref, far_up_ref, far_down_ref, up_out_ref, down_out_ref):
@@ -276,14 +287,23 @@
     down_out_ref[...] = (down_ref[...] + far_down_ref[...].astype(F32)).astype(BF16)
 
 
-def sum_body(own_ref, below_a_ref, below_b_ref, above_a_ref, above_b_ref, out_ref):
-    split = below_a_ref.shape[0]
-    for at, below, above in (
-        (slice(0, split), below_a_ref, above_a_ref),
-        (slice(split, own_ref.shape[0]), below_b_ref, above_b_ref),
-    ):
-        total = own_ref[at, :] + below[...].astype(F32) + above[...].astype(F32)
+CHUNKS = 4
+
+
+def sum_body(own_ref, below_a_ref, below_b_ref, above_a_ref, above_b_ref, out_hbm, out_ref, sems):
+    length, half = (own_ref.shape[0], below_a_ref.shape[0])
+    size = length // CHUNKS
+    copies = []
+    for i in range(CHUNKS):
+        at, start = slice(i * size, (i + 1) * size), i * size % half
+        part = slice(start, start + size)
+        below, above = (below_a_ref, above_a_ref) if i * size < half else (below_b_ref, above_b_ref)
+        total = own_ref[at, :] + below[part, :].astype(F32) + above[part, :].astype(F32)
         out_ref[at, :] = total.astype(BF16)
+        copies.append(pltpu.make_async_copy(out_ref.at[at], out_hbm.at[at], sems.at[i]))
+        copies[-1].start()
+    for copy in copies:
+        copy.wait()
 
 
 def ring(axis, shift):
@@ -342,19 +362,27 @@
     )
     keep, send = call(part_body, (state_half, state_half), entering, early, decay)
     other = lax.ppermute(send, "core", ring("core", 1))
-    kept, square = call(
-        keep_body, (shape((length, half), F32), shape((length, 1), F32)), keep, q_start, att_local
-    )
-    split = length // 2
-    first, last = shape((split, width), BF16), shape((length - split, width), BF16)
-    gated, far_up, far_down = call(
+    column = shape((length, 1), F32)
+    near = shape((length // 2, width), BF16)
+    near_f = shape((length // 2, width), F32)
+    kept, square, kept_far = call(
+        keep_body,
+        (shape((length, half), BF16), column, shape((length, width), F32)),
+        keep,
+        q_start,
+        att_local,
+        scale,
+        w_far,
+    )
+    gated, norm, far_up, far_down = call(
         finish_body,
-        (shape((length, DV), BF16), first, last),
+        (shape((length, DV), BF16), column, near, near),
         other,
         q_start,
         att_local,
         kept,
         square,
+        kept_far,
         scale,
         w_far,
     )
@@ -363,10 +391,11 @@
     far_down = lax.ppermute(far_down, "head", down)
     up_b, down_a = call(
         direct_body,
-        (last, first),
+        (near, near),
         gated,
+        norm,
         out_weight,
-        fetched=(1,),
+        fetched=(2,),
         scratch=[pltpu.VMEM((2, DV, width), BF16)],
         copies=2,
     )
@@ -374,18 +403,28 @@
     above_a = lax.ppermute(down_a, "head", down)
     up_a, down_b, own_part = call(
         near_body,
-        (shape(first.shape, F32), shape(last.shape, F32), shape((length, width), F32)),
+        (near_f, near_f, shape((length, width), F32)),
         gated,
+        norm,
         out_weight,
-        fetched=(1,),
+        fetched=(2,),
         scratch=[pltpu.VMEM((3, DV, width), BF16)],
         copies=3,
     )
-    up_a, down_b = call(pass_body, (first, last), up_a, down_b, far_up, far_down)
+    up_a, down_b = call(pass_body, (near, near), up_a, down_b, far_up, far_down)
     below_a = lax.ppermute(up_a, "head", up)
     above_b = lax.ppermute(down_b, "head", down)
     return call(
-        sum_body, shape((length, width), BF16), own_part, below_a, below_b, above_a, above_b
+        sum_body,
+        shape((length, width), BF16),
+        own_part,
+        below_a,
+        below_b,
+        above_a,
+        above_b,
+        scratch=[pltpu.VMEM((length, width), BF16)],
+        copies=CHUNKS,
+        outs_in=HBM,
     )
 
 

time: 66.8 us -> 66.3 us (level)
  no operation moved by 1% of the time
where the time goes in v4:
time: 66.3 us; the launch traced here: 65.7 us
  blocking collectives  23.3 us (35%)
  waiting for transfers between devices  16.8 us (25%)
  Pallas kernels  15.1 us (23%)
  starting transfers between devices  10.4 us (16%)
    all_to_all x1, blocking collectives, shards(): slices = lax.all_to_all(sent, CHIPS, 0, 0, tiled=True)  23.3 us
    pallas_call x12, Pallas kernels, call(): pl.pallas_call(body, out_shape=outs, in_specs=[HBM if i in fetched else V...  15.1 us
    all_to_all x1, waiting for transfers between devices, shards(): entering = lax.all_to_all(prefixes, CHIPS, 0, 0, tiled=True)  5.42 us
    all_to_all x1, starting transfers between devices, shards(): entering = lax.all_to_all(prefixes, CHIPS, 0, 0, tiled=True)  3.9 us
    ppermute x1, waiting for transfers between devices, shards(): below_a = lax.ppermute(up_a, 'head', up)  3.35 us
    ppermute x1, waiting for transfers between devices, shards(): below_b = lax.ppermute(up_b, 'head', up)  1.99 us
    ppermute x1, starting transfers between devices, shards(): far_down = lax.ppermute(far_down, 'head', down)  1.8 us
    ppermute x1, starting transfers between devices, shards(): above_b = lax.ppermute(down_b, 'head', down)  1.66 us
  transfers between devices with their start and end apart: 9, of which 8 were waited for; matrix products, arithmetic and copies ran while one was open for 0% of the time, Pallas kernels for 16%

profile of v4, /device:TPU:24, one launch (start us, length us, event | category | flops | bytes accessed | tf_op | source)
XLA Modules:
  0.0 65.7 jit_solution(8289745619556993057)
XLA Ops:
  0.0 1.7 %shard_map.73 = (bf16[528,128]{1,0:T(8,128)(2,1)S(1)}, f32[8,128]{1,0:T(8,128)S(1)}, bf16[512,256]{1,0:T(8,128)(2,1)S(1)}) custom-call(bf16[512,256]{1,0:T(8,128)(2,1)} %k_hbm.3, bf16[512,512]{1,0:T(8,128)(2,1)} %v_hbm.5, bf16[512,256]{1,0:T(8,128)(2,1)} %g_hbm.3), custom_call_target="tpu_custom_call" | custom-call | flops 1000000000 | bytes 1048576 | tf_op jit(solution)/shard_map/pallas_call | solution.py:33
  1.8 1.3 %shard_map.74.own_ref = f32[512,128]{1,0:T(8,128)S(1)} custom-call(bf16[512,512]{1,0:T(8,128)(2,1)} %v_hbm.5, bf16[512,256]{1,0:T(8,128)(2,1)S(1)} %get-tuple-element.38.state_ref), custom_call_target="tpu_custom_call" | custom-call | flops 1000000000 | bytes 786432 | tf_op jit(solution)/shard_map/pallas_call | solution.py:33
  3.3 23.3 %all_to_all.10.in_ref = bf16[32,24,128]{2,1,0:T(8,128)(2,1)S(1)} all-to-all(bf16[32,24,128]{2,1,0:T(8,128)(2,1)S(1)} %get-tuple-element.41), channel_id=1, replica_groups=mesh['chip_x'=4,'chip_z'=8,'core'=2,'head'=4] {'chip_x','chip_z'}, dimensions={0} | all-to-all | bytes 393216 | tf_op jit(solution)/shard_map/all_to_all | solution.py:339
  26.6 0.7 %shard_map.76 = bf16[32,16,128]{2,1,0:T(8,128)(2,1)} custom-call(bf16[32,24,128]{2,1,0:T(8,128)(2,1)S(1)} %all_to_all.10.in_ref), custom_call_target="tpu_custom_call" | custom-call | flops 1000000000 | bytes 196608 | tf_op jit(solution)/shard_map/pallas_call | solution.py:33
  27.3 3.9 %all-to-all-start.1 = ((bf16[32,16,128]{2,1,0:T(8,128)(2,1)}), bf16[32,16,128]{2,1,0:T(8,128)(2,1)S(1)}, u32[]{:S(2)}, u32[]{:S(2)}) async-start(bf16[32,16,128]{2,1,0:T(8,128)(2,1)} %shard_map.76), calls=%async_computation.1 | async-start | bytes 262144 | tf_op jit(solution)/shard_map/all_to_all | solution.py:358
  31.2 4.8 %shard_map.77 = (f32[512,512]{1,0:T(8,128)S(1)}, bf16[512,256]{1,0:T(8,128)(2,1)S(1)}, bf16[512,512]{1,0:T(8,128)(2,1)S(1)}, bf16[512,512]{1,0:T(8,128)(2,1)S(1)}) custom-call(bf16[512,256]{1,0:T(8,128)(2,1)} %q_hbm, bf16[512,256]{1,0:T(8,128)(2,1)} %k_hbm.3, bf16[512,512]{1,0:T(8,128)(2,1)} %v_hbm.5, bf16[512,256]{1,0:T(8,128)(2,1)} %g_hbm.3, ...), custom_call_target="tpu_custom_call" | custom-call | flops 1000000000 | bytes 3934208 | tf_op jit(solution)/shard_map/pallas_call | solution.py:33
  36.1 5.4 %all-to-all-done.1.in_ref = bf16[32,16,128]{2,1,0:T(8,128)(2,1)S(1)} async-done(((bf16[32,16,128]{2,1,0:T(8,128)(2,1)}), bf16[32,16,128]{2,1,0:T(8,128)(2,1)S(1)}, u32[]{:S(2)}, u32[]{:S(2)}) %all-to-all-start.1) | async-done | bytes 131104 | tf_op jit(solution)/shard_map/all_to_all | solution.py:358
  41.7 0.7 %shard_map.79 = (bf16[512,256]{1,0:T(8,128)(2,1)S(1)}, f32[512,1]{1,0:T(8,128)S(1)}, f32[512,512]{1,0:T(8,128)S(1)}) custom-call(bf16[512,128]{1,0:T(8,128)(2,1)S(1)} %get-tuple-element.54.keep_ref, bf16[512,256]{1,0:T(8,128)(2,1)S(1)} %get-tuple-element.52.q_ref, f32[512,512]{1,0:T(8,128)S(1)} %get-tuple-element.53.att_ref, ...), custom_call_target="tpu_custom_call" | custom-call | flops 1000000000 | bytes 2490368 | tf_op jit(solution)/shard_map/pallas_call | solution.py:33
  42.3 0.7 collective-permute-done.1.other_ref
  43.0 0.9 %shard_map.80 = (bf16[512,512]{1,0:T(8,128)(2,1)S(1)}, f32[512,1]{1,0:T(8,128)S(1)}, bf16[256,512]{1,0:T(8,128)(2,1)S(1)}, bf16[256,512]{1,0:T(8,128)(2,1)S(1)}) custom-call(bf16[512,128]{1,0:T(8,128)(2,1)S(1)} %collective-permute-done.1.other_ref, bf16[512,256]{1,0:T(8,128)(2,1)S(1)} %get-tuple-element.52.q_ref, f32[512,512]{1,0:T(8,128)S(1)} %get-tuple-element.53.att_ref, ...), custom_call_target="tpu_custom_call" | custom-call | flops 1000000000 | bytes 3803136 | tf_op jit(solution)/shard_map/pallas_call | solution.py:33
  44.2 1.8 %collective-permute-start.3 = (bf16[256,512]{1,0:T(8,128)(2,1)S(1)}, bf16[256,512]{1,0:T(8,128)(2,1)S(1)}, u32[]{:S(2)}, u32[]{:S(2)}) collective-permute-start(bf16[256,512]{1,0:T(8,128)(2,1)S(1)} %get-tuple-element.66), channel_id=1, source_target_pairs={{0,3},{1,0},{2,1},{3,2},{4,7},{5,4},{6,5},{7,6},{8,11},{9,8},{10,9... | collective-permute-start | bytes 786440 | tf_op jit(solution)/shard_map/ppermute | solution.py:391
  46.0 1.7 %shard_map.83 = (bf16[256,512]{1,0:T(8,128)(2,1)S(1)}, bf16[256,512]{1,0:T(8,128)(2,1)S(1)}) custom-call(bf16[512,512]{1,0:T(8,128)(2,1)S(1)} %get-tuple-element.60.gated_ref, f32[512,1]{1,0:T(8,128)S(1)} %get-tuple-element.61.norm_ref, bf16[512,2048]{1,0:T(8,128)(2,1)} %w_hbm.5), custom_call_target="tpu_custom_call" | custom-call | flops 1000000000 | bytes 2623488 | tf_op jit(solution)/shard_map/pallas_call | solution.py:33
  47.7 1.5 %collective-permute-start.5 = (bf16[256,512]{1,0:T(8,128)(2,1)S(1)}, bf16[256,512]{1,0:T(8,128)(2,1)S(1)}, u32[]{:S(2)}, u32[]{:S(2)}) collective-permute-start(bf16[256,512]{1,0:T(8,128)(2,1)S(1)} %get-tuple-element.68), channel_id=1, source_target_pairs={{0,1},{1,2},{2,3},{3,0},{4,5},{5,6},{6,7},{7,4},{8,9},{9,10},{10,1... | collective-permute-start | bytes 786440 | tf_op jit(solution)/shard_map/ppermute | solution.py:402
  49.2 0.6 collective-permute-start.6
  49.8 2.1 %shard_map.81 = (f32[256,512]{1,0:T(8,128)S(1)}, f32[256,512]{1,0:T(8,128)S(1)}, f32[512,512]{1,0:T(8,128)S(1)}) custom-call(bf16[512,512]{1,0:T(8,128)(2,1)S(1)} %get-tuple-element.60.gated_ref, f32[512,1]{1,0:T(8,128)S(1)} %get-tuple-element.61.norm_ref, bf16[512,2048]{1,0:T(8,128)(2,1)} %w_hbm.5), custom_call_target="tpu_custom_call" | custom-call | flops 1000000000 | bytes 2623488 | tf_op jit(solution)/shard_map/pallas_call | solution.py:33
  51.9 1.3 %collective-permute-done.2.far_up_ref = bf16[256,512]{1,0:T(8,128)(2,1)S(1)} collective-permute-done((bf16[256,512]{1,0:T(8,128)(2,1)S(1)}, bf16[256,512]{1,0:T(8,128)(2,1)S(1)}, u32[]{:S(2)}, u32[]{:S(2)}) %collective-permute-start.2) | collective-permute-done | bytes 262176 | tf_op jit(solution)/shard_map/ppermute | solution.py:390
  53.1 1.4 %collective-permute-done.3.far_down_ref = bf16[256,512]{1,0:T(8,128)(2,1)S(1)} collective-permute-done((bf16[256,512]{1,0:T(8,128)(2,1)S(1)}, bf16[256,512]{1,0:T(8,128)(2,1)S(1)}, u32[]{:S(2)}, u32[]{:S(2)}) %collective-permute-start.3) | collective-permute-done | bytes 262176 | tf_op jit(solution)/shard_map/ppermute | solution.py:391
  54.7 0.4 collective-permute-start.4
  55.1 1.7 %collective-permute-start.7 = (bf16[256,512]{1,0:T(8,128)(2,1)S(1)}, bf16[256,512]{1,0:T(8,128)(2,1)S(1)}, u32[]{:S(2)}, u32[]{:S(2)}) collective-permute-start(bf16[256,512]{1,0:T(8,128)(2,1)S(1)} %get-tuple-element.70), channel_id=1, source_target_pairs={{0,3},{1,0},{2,1},{3,2},{4,7},{5,4},{6,5},{7,6},{8,11},{9,8},{10,9... | collective-permute-start | bytes 786440 | tf_op jit(solution)/shard_map/ppermute | solution.py:416
  56.8 2.0 %collective-permute-done.5.below_b_ref = bf16[256,512]{1,0:T(8,128)(2,1)S(1)} collective-permute-done((bf16[256,512]{1,0:T(8,128)(2,1)S(1)}, bf16[256,512]{1,0:T(8,128)(2,1)S(1)}, u32[]{:S(2)}, u32[]{:S(2)}) %collective-permute-start.5) | collective-permute-done | bytes 262176 | tf_op jit(solution)/shard_map/ppermute | solution.py:402
  58.8 1.4 %collective-permute-done.6.above_a_ref = bf16[256,512]{1,0:T(8,128)(2,1)S(1)} collective-permute-done((bf16[256,512]{1,0:T(8,128)(2,1)S(1)}, bf16[256,512]{1,0:T(8,128)(2,1)S(1)}, u32[]{:S(2)}, u32[]{:S(2)}) %collective-permute-start.6) | collective-permute-done | bytes 262176 | tf_op jit(solution)/shard_map/ppermute | solution.py:403
  60.2 3.4 %collective-permute-done.4.below_a_ref = bf16[256,512]{1,0:T(8,128)(2,1)S(1)} collective-permute-done((bf16[256,512]{1,0:T(8,128)(2,1)S(1)}, bf16[256,512]{1,0:T(8,128)(2,1)S(1)}, u32[]{:S(2)}, u32[]{:S(2)}) %collective-permute-start.4) | collective-permute-done | bytes 262176 | tf_op jit(solution)/shard_map/ppermute | solution.py:415
  63.5 1.3 %collective-permute-done.7.above_b_ref = bf16[256,512]{1,0:T(8,128)(2,1)S(1)} collective-permute-done((bf16[256,512]{1,0:T(8,128)(2,1)S(1)}, bf16[256,512]{1,0:T(8,128)(2,1)S(1)}, u32[]{:S(2)}, u32[]{:S(2)}) %collective-permute-start.7) | collective-permute-done | bytes 262176 | tf_op jit(solution)/shard_map/ppermute | solution.py:416
  64.8 0.9 %shard_map.84 = bf16[512,512]{1,0:T(8,128)(2,1)} custom-call(f32[512,512]{1,0:T(8,128)S(1)} %get-tuple-element.62.own_ref, bf16[256,512]{1,0:T(8,128)(2,1)S(1)} %collective-permute-done.4.below_a_ref, bf16[256,512]{1,0:T(8,128)(2,1)S(1)} %collective-permute-done.5.below_b_ref, bf16[256,512]{1,0:T(8,128)(2,1)S(1)} %collective-permute-done.6.above_a_ref, ...), custom_call_target="tpu_custom_call" | custom-call | flops 1000000000 | bytes 2097152 | tf_op jit(solution)/shard_map/pallas_call | solution.py:33
  (9 shorter events, 0.7 us)
Async XLA Ops:
  1.7 1.4 %collective-permute-start = (bf16[528,128]{1,0:T(8,128)(2,1)S(1)}, bf16[528,128]{1,0:T(8,128)(2,1)S(1)}, u32[]{:S(2)}, u32[]{:S(2)}) collective-permute-start(bf16[528,128]{1,0:T(8,128)(2,1)S(1)} %get-tuple-element.40), channel_id=1, source_target_pairs={{0,4},{4,0},{1,5},{5,1},{2,6},{6,2},{3,7},{7,3},{8,12},{12,8},{9,1... | collective-permute-start | bytes 405512 | tf_op jit(solution)/shard_map/ppermute | solution.py:330
  3.2 28.0 %copy-start = (f32[512]{0:T(512)S(1)}, f32[512]{0:T(512)}, u32[]{:S(2)}) copy-start(f32[512]{0:T(512)} %param.12) | copy-start | bytes 6148
  27.3 14.2 %all-to-all-start.1 = ((bf16[32,16,128]{2,1,0:T(8,128)(2,1)}), bf16[32,16,128]{2,1,0:T(8,128)(2,1)S(1)}, u32[]{:S(2)}, u32[]{:S(2)}) async-start(bf16[32,16,128]{2,1,0:T(8,128)(2,1)} %shard_map.76), calls=%async_computation.1 | async-start | bytes 262144 | tf_op jit(solution)/shard_map/all_to_all | solution.py:358
  41.6 1.4 %collective-permute-start.1 = (bf16[512,128]{1,0:T(8,128)(2,1)S(1)}, bf16[512,128]{1,0:T(8,128)(2,1)S(1)}, u32[]{:S(2)}, u32[]{:S(2)}) collective-permute-start(bf16[512,128]{1,0:T(8,128)(2,1)S(1)} %get-tuple-element.51), channel_id=1, source_target_pairs={{0,4},{4,0},{1,5},{5,1},{2,6},{6,2},{3,7},{7,3},{8,12},{12,8},{9,1... | collective-permute-start | bytes 393224 | tf_op jit(solution)/shard_map/ppermute | solution.py:364
  43.9 9.2 %collective-permute-start.2 = (bf16[256,512]{1,0:T(8,128)(2,1)S(1)}, bf16[256,512]{1,0:T(8,128)(2,1)S(1)}, u32[]{:S(2)}, u32[]{:S(2)}) collective-permute-start(bf16[256,512]{1,0:T(8,128)(2,1)S(1)} %get-tuple-element.65), channel_id=1, source_target_pairs={{0,1},{1,2},{2,3},{3,0},{4,5},{5,6},{6,7},{7,4},{8,9},{9,10},{10,1... | collective-permute-start | bytes 786440 | tf_op jit(solution)/shard_map/ppermute | solution.py:390
  44.2 10.4 %collective-permute-start.3 = (bf16[256,512]{1,0:T(8,128)(2,1)S(1)}, bf16[256,512]{1,0:T(8,128)(2,1)S(1)}, u32[]{:S(2)}, u32[]{:S(2)}) collective-permute-start(bf16[256,512]{1,0:T(8,128)(2,1)S(1)} %get-tuple-element.66), channel_id=1, source_target_pairs={{0,3},{1,0},{2,1},{3,2},{4,7},{5,4},{6,5},{7,6},{8,11},{9,8},{10,9... | collective-permute-start | bytes 786440 | tf_op jit(solution)/shard_map/ppermute | solution.py:391
  47.7 11.1 %collective-permute-start.5 = (bf16[256,512]{1,0:T(8,128)(2,1)S(1)}, bf16[256,512]{1,0:T(8,128)(2,1)S(1)}, u32[]{:S(2)}, u32[]{:S(2)}) collective-permute-start(bf16[256,512]{1,0:T(8,128)(2,1)S(1)} %get-tuple-element.68), channel_id=1, source_target_pairs={{0,1},{1,2},{2,3},{3,0},{4,5},{5,6},{6,7},{7,4},{8,9},{9,10},{10,1... | collective-permute-start | bytes 786440 | tf_op jit(solution)/shard_map/ppermute | solution.py:402
  49.2 11.0 %collective-permute-start.6 = (bf16[256,512]{1,0:T(8,128)(2,1)S(1)}, bf16[256,512]{1,0:T(8,128)(2,1)S(1)}, u32[]{:S(2)}, u32[]{:S(2)}) collective-permute-start(bf16[256,512]{1,0:T(8,128)(2,1)S(1)} %get-tuple-element.69), channel_id=1, source_target_pairs={{0,3},{1,0},{2,1},{3,2},{4,7},{5,4},{6,5},{7,6},{8,11},{9,8},{10,9... | collective-permute-start | bytes 786440 | tf_op jit(solution)/shard_map/ppermute | solution.py:403
  54.7 8.9 %collective-permute-start.4 = (bf16[256,512]{1,0:T(8,128)(2,1)S(1)}, bf16[256,512]{1,0:T(8,128)(2,1)S(1)}, u32[]{:S(2)}, u32[]{:S(2)}) collective-permute-start(bf16[256,512]{1,0:T(8,128)(2,1)S(1)} %get-tuple-element.67), channel_id=1, source_target_pairs={{0,1},{1,2},{2,3},{3,0},{4,5},{5,6},{6,7},{7,4},{8,9},{9,10},{10,1... | collective-permute-start | bytes 786440 | tf_op jit(solution)/shard_map/ppermute | solution.py:415
  55.1 9.7 %collective-permute-start.7 = (bf16[256,512]{1,0:T(8,128)(2,1)S(1)}, bf16[256,512]{1,0:T(8,128)(2,1)S(1)}, u32[]{:S(2)}, u32[]{:S(2)}) collective-permute-start(bf16[256,512]{1,0:T(8,128)(2,1)S(1)} %get-tuple-element.70), channel_id=1, source_target_pairs={{0,3},{1,0},{2,1},{3,2},{4,7},{5,4},{6,5},{7,6},{8,11},{9,8},{10,9... | collective-permute-start | bytes 786440 | tf_op jit(solution)/shard_map/ppermute | solution.py:416

commit v5 on v4

--- a/solution.py
+++ b/solution.py
@@ -1,3 +1,5 @@
+import functools
+
 import jax
 import jax.numpy as jnp
 from jax import lax
@@ -81,9 +83,10 @@
 
 
 def swap_body(k_hbm, v_hbm, g_hbm, swap_ref, log_ref, state_ref, k_ref, v_ref, g_ref, sems):
-    gate_copy, k_copy, v_copy = fetch(sems, (g_hbm, g_ref), (k_hbm, k_ref), (v_hbm, v_ref))
+    half = DV // 2
+    theirs = v_hbm.at[:, columns(1 - lax.axis_index("core"), half)]
+    gate_copy, k_copy, v_copy = fetch(sems, (g_hbm, g_ref), (k_hbm, k_ref), (theirs, v_ref))
     length = k_ref.shape[0]
-    half = DV // 2
     mask = triangle(length, lambda r, c: c > r)
     gate_copy.wait()
     gate = g_ref[...]
@@ -93,8 +96,7 @@
     v_copy.wait()
     k_state = (k_ref[...].astype(F32) * jnp.exp(after)).astype(BF16)
     state_ref[...] = k_state
-    theirs = columns(1 - lax.axis_index("core"), half)
-    state = dot(v_ref[:, theirs], k_state, ((0,), (0,))).astype(BF16)
+    state = dot(v_ref[...], k_state, ((0,), (0,))).astype(BF16)
     swap_ref[0:half, :] = state[:, :LANE]
     swap_ref[half : 2 * half, :] = state[:, LANE:]
     left_high, left_low = split_bf16(total[:, :LANE])
@@ -105,11 +107,11 @@
 
 
 def own_body(v_hbm, state_ref, own_ref, v_ref, sems):
-    (copy,) = fetch(sems, (v_hbm, v_ref))
+    half = DV // 2
+    mine = v_hbm.at[:, columns(lax.axis_index("core"), half)]
+    (copy,) = fetch(sems, (mine, v_ref))
     copy.wait()
-    half = DV // 2
-    mine = columns(lax.axis_index("core"), half)
-    state = dot(v_ref[:, mine], state_ref[...], ((0,), (0,)))
+    state = dot(v_ref[...], state_ref[...], ((0,), (0,)))
     own_ref[0:half, :] = state[:, :LANE]
     own_ref[half:, :] = state[:, LANE:]
 
@@ -232,26 +234,24 @@
 
 
 def finish_body(
-    other_ref, q_ref, att_ref, kept_ref, square_ref, kept_far_ref, scale_ref, w_ref,
-    gated_ref, norm_ref, far_up_ref, far_down_ref,
+    row, other_ref, q_ref, att_ref, kept_ref, square_ref, kept_far_ref, scale_ref, w_ref,
+    gated_ref, norm_ref, far_ref,
 ):
     half = other_ref.shape[0] // 2
     core = lax.axis_index("core")
     here, there = columns(core, half), columns(1 - core, half)
-    attention = att_ref[:, there]
-    attention = attention + dot(q_ref[:, :LANE], other_ref[:half, :], ((1,), (1,)))
-    attention = attention + dot(q_ref[:, LANE:], other_ref[half:, :], ((1,), (1,)))
-    gated = (attention * scale_ref[:, there].astype(F32)).astype(BF16)
-    far = kept_far_ref[...] + dot(gated, w_ref[there, :])
-    total = square_ref[...] + jnp.sum(attention * attention, axis=-1, keepdims=True)
+    at = slice(row, row + far_ref.shape[0])
+    attention = att_ref[at, there]
+    attention = attention + dot(q_ref[at, :LANE], other_ref[:half, :], ((1,), (1,)))
+    attention = attention + dot(q_ref[at, LANE:], other_ref[half:, :], ((1,), (1,)))
+    gated = (attention * scale_ref[at, there].astype(F32)).astype(BF16)
+    far = kept_far_ref[at, :] + dot(gated, w_ref[there, :])
+    total = square_ref[at, :] + jnp.sum(attention * attention, axis=-1, keepdims=True)
     norm = lax.rsqrt(total * (1.0 / DV) + 1e-05)
     norm_ref[...] = norm
-    far = (far * norm).astype(BF16)
-    split = far_up_ref.shape[0]
-    far_up_ref[...] = far[:split]
-    far_down_ref[...] = far[split:]
+    far_ref[...] = (far * norm).astype(BF16)
     gated_ref[:, there] = gated
-    gated_ref[:, here] = kept_ref[...]
+    gated_ref[:, here] = kept_ref[at, :]
 
 
 def fetch_columns(w_hbm, w_ref, sems, *shifts):
@@ -260,26 +260,26 @@
     return fetch(sems, *pairs)
 
 
-def direct_body(gated_ref, norm_ref, w_hbm, up_ref, down_ref, w_ref, sems):
+def direct_body(top_ref, low_ref, norm_top_ref, norm_low_ref, w_hbm, up_ref, down_ref, w_ref, sems):
     copies = fetch_columns(w_hbm, w_ref, sems, 1, 3)
-    half = up_ref.shape[0]
-    top, low = slice(0, half), slice(half, 2 * half)
     copies[0].wait()
-    up_ref[...] = (dot(gated_ref[low, :], w_ref[0]) * norm_ref[low, :]).astype(BF16)
+    up_ref[...] = (dot(low_ref[...], w_ref[0]) * norm_low_ref[...]).astype(BF16)
     copies[1].wait()
-    down_ref[...] = (dot(gated_ref[top, :], w_ref[1]) * norm_ref[top, :]).astype(BF16)
-
-
-def near_body(gated_ref, norm_ref, w_hbm, up_ref, down_ref, own_ref, w_ref, sems):
+    down_ref[...] = (dot(top_ref[...], w_ref[1]) * norm_top_ref[...]).astype(BF16)
+
+
+def near_body(
+    top_ref, low_ref, norm_top_ref, norm_low_ref, w_hbm, up_ref, down_ref, own_ref, w_ref, sems
+):
     copies = fetch_columns(w_hbm, w_ref, sems, 1, 3, 0)
     half = up_ref.shape[0]
-    top, low = slice(0, half), slice(half, 2 * half)
     copies[0].wait()
-    up_ref[...] = dot(gated_ref[top, :], w_ref[0]) * norm_ref[top, :]
+    up_ref[...] = dot(top_ref[...], w_ref[0]) * norm_top_ref[...]
     copies[1].wait()
-    down_ref[...] = dot(gated_ref[low, :], w_ref[1]) * norm_ref[low, :]
+    down_ref[...] = dot(low_ref[...], w_ref[1]) * norm_low_ref[...]
     copies[2].wait()
-    own_ref[...] = dot(gated_ref[...], w_ref[2]) * norm_ref[...]
+    own_ref[:half, :] = dot(top_ref[...], w_ref[2]) * norm_top_ref[...]
+    own_ref[half:, :] = dot(low_ref[...], w_ref[2]) * norm_low_ref[...]
 
 
 def pass_body(up_ref, down_ref, far_up_ref, far_down_ref, up_out_ref, down_out_ref):
@@ -326,9 +326,19 @@
         values,
         log_gate,
         fetched=(0, 1, 2),
+        scratch=[pltpu.VMEM((length, n), BF16) for n in (DK, half, DK)],
+        copies=3,
     )
     swapped = lax.ppermute(swap, "core", ring("core", 1))
-    own = call(own_body, shape((DV, LANE), F32), values, k_state, fetched=(0,))
+    own = call(
+        own_body,
+        shape((DV, LANE), F32),
+        values,
+        k_state,
+        fetched=(0,),
+        scratch=[pltpu.VMEM((length, half), BF16)],
+        copies=1,
+    )
     sent, early, decay = call(
         join_body,
         (shape((pieces, 2 * rows + 8, LANE), BF16), shape((DV, LANE), BF16), small),
@@ -374,28 +384,22 @@
         scale,
         w_far,
     )
-    gated, norm, far_up, far_down = call(
-        finish_body,
-        (shape((length, DV), BF16), column, near, near),
-        other,
-        q_start,
-        att_local,
-        kept,
-        square,
-        kept_far,
-        scale,
-        w_far,
-    )
     up, down = ring("head", 1), ring("head", -1)
+    rows_out = (shape((length // 2, DV), BF16), shape((length // 2, 1), F32), near)
+    finish_in = (other, q_start, att_local, kept, square, kept_far, scale, w_far)
+    top, norm_top, far_up = call(functools.partial(finish_body, 0), rows_out, *finish_in)
     far_up = lax.ppermute(far_up, "head", up)
+    low, norm_low, far_down = call(
+        functools.partial(finish_body, length // 2), rows_out, *finish_in
+    )
     far_down = lax.ppermute(far_down, "head", down)
+    gated = (top, low, norm_top, norm_low)
     up_b, down_a = call(
         direct_body,
         (near, near),
-        gated,
-        norm,
+        *gated,
         out_weight,
-        fetched=(2,),
+        fetched=(4,),
         scratch=[pltpu.VMEM((2, DV, width), BF16)],
         copies=2,
     )
@@ -404,10 +408,9 @@
     up_a, down_b, own_part = call(
         near_body,
         (near_f, near_f, shape((length, width), F32)),
-        gated,
-        norm,
+        *gated,
         out_weight,
-        fetched=(2,),
+        fetched=(4,),
         scratch=[pltpu.VMEM((3, DV, width), BF16)],
         copies=3,
     )

time: 66.3 us -> 68.8 us (1.038)
  the two profiles are of different devices: /device:TPU:24 before, /device:TPU:1 now
where the time goes in v5:
time: 68.8 us; the launch traced here: 68.5 us
  starting transfers between devices  20 us (29%)
  blocking collectives  18.5 us (27%)
  Pallas kernels  15 us (22%)
  waiting for transfers between devices  14.8 us (22%)
    all_to_all x1, blocking collectives, shards(): slices = lax.all_to_all(sent, CHIPS, 0, 0, tiled=True)  18.5 us
    pallas_call x13, Pallas kernels, call(): pl.pallas_call(body, out_shape=outs, in_specs=[HBM if i in fetched else V...  15 us
    all_to_all x1, starting transfers between devices, shards(): entering = lax.all_to_all(prefixes, CHIPS, 0, 0, tiled=True)  5.7 us
    ppermute x1, waiting for transfers between devices, shards(): below_a = lax.ppermute(up_a, 'head', up)  5.61 us
    all_to_all x1, waiting for transfers between devices, shards(): entering = lax.all_to_all(prefixes, CHIPS, 0, 0, tiled=True)  4.31 us
    ppermute x1, starting transfers between devices, shards(): swapped = lax.ppermute(swap, 'core', ring('core', 1))  3.29 us
    ppermute x1, starting transfers between devices, shards(): far_down = lax.ppermute(far_down, 'head', down)  2.81 us
    ppermute x1, waiting for transfers between devices, shards(): below_b = lax.ppermute(up_b, 'head', up)  2.77 us
  transfers between devices with their start and end apart: 9, of which 5 were waited for; matrix products, arithmetic and copies ran while one was open for 0% of the time, Pallas kernels for 16%

profile of v5, /device:TPU:1, one launch (start us, length us, event | category | flops | bytes accessed | tf_op | source)
XLA Modules:
  0.0 68.5 jit_solution(3644877474909791956)
XLA Ops:
  0.0 1.7 %shard_map.73 = (bf16[528,128]{1,0:T(8,128)(2,1)S(1)}, f32[8,128]{1,0:T(8,128)S(1)}, bf16[512,256]{1,0:T(8,128)(2,1)S(1)}) custom-call(bf16[512,256]{1,0:T(8,128)(2,1)} %k_hbm.3, bf16[512,512]{1,0:T(8,128)(2,1)} %v_hbm.5, bf16[512,256]{1,0:T(8,128)(2,1)} %g_hbm.3), custom_call_target="tpu_custom_call" | custom-call | flops 1000000000 | bytes 1048576 | tf_op jit(solution)/shard_map/pallas_call | solution.py:35
  1.7 3.3 %collective-permute-start = (bf16[528,128]{1,0:T(8,128)(2,1)S(1)}, bf16[528,128]{1,0:T(8,128)(2,1)S(1)}, u32[]{:S(2)}, u32[]{:S(2)}) collective-permute-start(bf16[528,128]{1,0:T(8,128)(2,1)S(1)} %get-tuple-element.42), channel_id=1, source_target_pairs={{0,4},{4,0},{1,5},{5,1},{2,6},{6,2},{3,7},{7,3},{8,12},{12,8},{9,1... | collective-permute-start | bytes 405512 | tf_op jit(solution)/shard_map/ppermute | solution.py:332
  5.0 1.2 %shard_map.74.own_ref = f32[512,128]{1,0:T(8,128)S(1)} custom-call(bf16[512,512]{1,0:T(8,128)(2,1)} %v_hbm.5, bf16[512,256]{1,0:T(8,128)(2,1)S(1)} %get-tuple-element.40.state_ref), custom_call_target="tpu_custom_call" | custom-call | flops 1000000000 | bytes 786432 | tf_op jit(solution)/shard_map/pallas_call | solution.py:35
  6.2 0.1 shard_map.75
  6.3 18.5 %all_to_all.10.in_ref = bf16[32,24,128]{2,1,0:T(8,128)(2,1)S(1)} all-to-all(bf16[32,24,128]{2,1,0:T(8,128)(2,1)S(1)} %get-tuple-element.43), channel_id=1, replica_groups=mesh['chip_x'=4,'chip_z'=8,'core'=2,'head'=4] {'chip_x','chip_z'}, dimensions={0} | all-to-all | bytes 393216 | tf_op jit(solution)/shard_map/all_to_all | solution.py:349
  24.9 0.7 %shard_map.76 = bf16[32,16,128]{2,1,0:T(8,128)(2,1)} custom-call(bf16[32,24,128]{2,1,0:T(8,128)(2,1)S(1)} %all_to_all.10.in_ref), custom_call_target="tpu_custom_call" | custom-call | flops 1000000000 | bytes 196608 | tf_op jit(solution)/shard_map/pallas_call | solution.py:35
  25.6 5.7 %all-to-all-start.1 = ((bf16[32,16,128]{2,1,0:T(8,128)(2,1)}), bf16[32,16,128]{2,1,0:T(8,128)(2,1)S(1)}, u32[]{:S(2)}, u32[]{:S(2)}) async-start(bf16[32,16,128]{2,1,0:T(8,128)(2,1)} %shard_map.76), calls=%async_computation.1 | async-start | bytes 262144 | tf_op jit(solution)/shard_map/all_to_all | solution.py:368
  31.3 4.8 %shard_map.77 = (f32[512,512]{1,0:T(8,128)S(1)}, bf16[512,256]{1,0:T(8,128)(2,1)S(1)}, bf16[512,512]{1,0:T(8,128)(2,1)S(1)}, bf16[512,512]{1,0:T(8,128)(2,1)S(1)}) custom-call(bf16[512,256]{1,0:T(8,128)(2,1)} %q_hbm, bf16[512,256]{1,0:T(8,128)(2,1)} %k_hbm.3, bf16[512,512]{1,0:T(8,128)(2,1)} %v_hbm.5, bf16[512,256]{1,0:T(8,128)(2,1)} %g_hbm.3, ...), custom_call_target="tpu_custom_call" | custom-call | flops 1000000000 | bytes 3934208 | tf_op jit(solution)/shard_map/pallas_call | solution.py:35
  36.1 4.3 %all-to-all-done.1.in_ref = bf16[32,16,128]{2,1,0:T(8,128)(2,1)S(1)} async-done(((bf16[32,16,128]{2,1,0:T(8,128)(2,1)}), bf16[32,16,128]{2,1,0:T(8,128)(2,1)S(1)}, u32[]{:S(2)}, u32[]{:S(2)}) %all-to-all-start.1) | async-done | bytes 131104 | tf_op jit(solution)/shard_map/all_to_all | solution.py:368
  40.5 2.6 %collective-permute-start.1 = (bf16[512,128]{1,0:T(8,128)(2,1)S(1)}, bf16[512,128]{1,0:T(8,128)(2,1)S(1)}, u32[]{:S(2)}, u32[]{:S(2)}) collective-permute-start(bf16[512,128]{1,0:T(8,128)(2,1)S(1)} %get-tuple-element.53), channel_id=1, source_target_pairs={{0,4},{4,0},{1,5},{5,1},{2,6},{6,2},{3,7},{7,3},{8,12},{12,8},{9,1... | collective-permute-start | bytes 393224 | tf_op jit(solution)/shard_map/ppermute | solution.py:374
  43.1 0.7 shard_map.79
  43.8 0.3 collective-permute-done.1.other_ref
  44.1 0.5 shard_map.81
  44.6 2.8 %collective-permute-start.3 = (bf16[256,512]{1,0:T(8,128)(2,1)S(1)}, bf16[256,512]{1,0:T(8,128)(2,1)S(1)}, u32[]{:S(2)}, u32[]{:S(2)}) collective-permute-start(bf16[256,512]{1,0:T(8,128)(2,1)S(1)} %get-tuple-element.70), channel_id=1, source_target_pairs={{0,3},{1,0},{2,1},{3,2},{4,7},{5,4},{6,5},{7,6},{8,11},{9,8},{10,9... | collective-permute-start | bytes 786440 | tf_op jit(solution)/shard_map/ppermute | solution.py:395
  47.4 0.5 shard_map.80
  48.0 1.7 %shard_map.84 = (bf16[256,512]{1,0:T(8,128)(2,1)S(1)}, bf16[256,512]{1,0:T(8,128)(2,1)S(1)}) custom-call(bf16[256,512]{1,0:T(8,128)(2,1)S(1)} %get-tuple-element.62.top_ref, bf16[256,512]{1,0:T(8,128)(2,1)S(1)} %get-tuple-element.63.low_ref, f32[256,1]{1,0:T(8,128)S(1)} %get-tuple-element.64.norm_top_ref, f32[256,1]{1,0:T(8,128)S(1)} %get-tuple-element.65.norm_low_ref, ...), custom_call_target="tpu_custom_call" | custom-call | flops 1000000000 | bytes 2623488 | tf_op jit(solution)/shard_map/pallas_call | solution.py:35
  49.8 2.7 %collective-permute-start.6 = (bf16[256,512]{1,0:T(8,128)(2,1)S(1)}, bf16[256,512]{1,0:T(8,128)(2,1)S(1)}, u32[]{:S(2)}, u32[]{:S(2)}) collective-permute-start(bf16[256,512]{1,0:T(8,128)(2,1)S(1)} %get-tuple-element.73), channel_id=1, source_target_pairs={{0,3},{1,0},{2,1},{3,2},{4,7},{5,4},{6,5},{7,6},{8,11},{9,8},{10,9... | collective-permute-start | bytes 786440 | tf_op jit(solution)/shard_map/ppermute | solution.py:407
  52.5 2.1 %shard_map.82 = (f32[256,512]{1,0:T(8,128)S(1)}, f32[256,512]{1,0:T(8,128)S(1)}, f32[512,512]{1,0:T(8,128)S(1)}) custom-call(bf16[256,512]{1,0:T(8,128)(2,1)S(1)} %get-tuple-element.62.top_ref, bf16[256,512]{1,0:T(8,128)(2,1)S(1)} %get-tuple-element.63.low_ref, f32[256,1]{1,0:T(8,128)S(1)} %get-tuple-element.64.norm_top_ref, ...), custom_call_target="tpu_custom_call" | custom-call | flops 1000000000 | bytes 2623488 | tf_op jit(solution)/shard_map/pallas_call | solution.py:35
  54.7 1.8 %collective-permute-done.2.far_up_ref = bf16[256,512]{1,0:T(8,128)(2,1)S(1)} collective-permute-done((bf16[256,512]{1,0:T(8,128)(2,1)S(1)}, bf16[256,512]{1,0:T(8,128)(2,1)S(1)}, u32[]{:S(2)}, u32[]{:S(2)}) %collective-permute-start.2) | collective-permute-done | bytes 262176 | tf_op jit(solution)/shard_map/ppermute | solution.py:391
  56.4 0.1 shard_map.83
  56.6 2.7 %collective-permute-start.7 = (bf16[256,512]{1,0:T(8,128)(2,1)S(1)}, bf16[256,512]{1,0:T(8,128)(2,1)S(1)}, u32[]{:S(2)}, u32[]{:S(2)}) collective-permute-start(bf16[256,512]{1,0:T(8,128)(2,1)S(1)} %get-tuple-element.74), channel_id=1, source_target_pairs={{0,3},{1,0},{2,1},{3,2},{4,7},{5,4},{6,5},{7,6},{8,11},{9,8},{10,9... | collective-permute-start | bytes 786440 | tf_op jit(solution)/shard_map/ppermute | solution.py:419
  59.3 2.8 %collective-permute-done.5.below_b_ref = bf16[256,512]{1,0:T(8,128)(2,1)S(1)} collective-permute-done((bf16[256,512]{1,0:T(8,128)(2,1)S(1)}, bf16[256,512]{1,0:T(8,128)(2,1)S(1)}, u32[]{:S(2)}, u32[]{:S(2)}) %collective-permute-start.5) | collective-permute-done | bytes 262176 | tf_op jit(solution)/shard_map/ppermute | solution.py:406
  62.0 5.6 %collective-permute-done.4.below_a_ref = bf16[256,512]{1,0:T(8,128)(2,1)S(1)} collective-permute-done((bf16[256,512]{1,0:T(8,128)(2,1)S(1)}, bf16[256,512]{1,0:T(8,128)(2,1)S(1)}, u32[]{:S(2)}, u32[]{:S(2)}) %collective-permute-start.4) | collective-permute-done | bytes 262176 | tf_op jit(solution)/shard_map/ppermute | solution.py:418
  67.7 0.9 %shard_map.85 = bf16[512,512]{1,0:T(8,128)(2,1)} custom-call(f32[512,512]{1,0:T(8,128)S(1)} %get-tuple-element.66.own_ref, bf16[256,512]{1,0:T(8,128)(2,1)S(1)} %collective-permute-done.4.below_a_ref, bf16[256,512]{1,0:T(8,128)(2,1)S(1)} %collective-permute-done.5.below_b_ref, bf16[256,512]{1,0:T(8,128)(2,1)S(1)} %collective-permute-done.6.above_a_ref, ...), custom_call_target="tpu_custom_call" | custom-call | flops 1000000000 | bytes 2097152 | tf_op jit(solution)/shard_map/pallas_call | solution.py:35
  (10 shorter events, 0.3 us)
Async XLA Ops:
  1.7 4.5 %collective-permute-start = (bf16[528,128]{1,0:T(8,128)(2,1)S(1)}, bf16[528,128]{1,0:T(8,128)(2,1)S(1)}, u32[]{:S(2)}, u32[]{:S(2)}) collective-permute-start(bf16[528,128]{1,0:T(8,128)(2,1)S(1)} %get-tuple-element.42), channel_id=1, source_target_pairs={{0,4},{4,0},{1,5},{5,1},{2,6},{6,2},{3,7},{7,3},{8,12},{12,8},{9,1... | collective-permute-start | bytes 405512 | tf_op jit(solution)/shard_map/ppermute | solution.py:332
  6.3 25.0 %copy-start = (f32[512]{0:T(512)S(1)}, f32[512]{0:T(512)}, u32[]{:S(2)}) copy-start(f32[512]{0:T(512)} %param.12) | copy-start | bytes 6148
  25.6 14.9 %all-to-all-start.1 = ((bf16[32,16,128]{2,1,0:T(8,128)(2,1)}), bf16[32,16,128]{2,1,0:T(8,128)(2,1)S(1)}, u32[]{:S(2)}, u32[]{:S(2)}) async-start(bf16[32,16,128]{2,1,0:T(8,128)(2,1)} %shard_map.76), calls=%async_computation.1 | async-start | bytes 262144 | tf_op jit(solution)/shard_map/all_to_all | solution.py:368
  40.5 3.6 %collective-permute-start.1 = (bf16[512,128]{1,0:T(8,128)(2,1)S(1)}, bf16[512,128]{1,0:T(8,128)(2,1)S(1)}, u32[]{:S(2)}, u32[]{:S(2)}) collective-permute-start(bf16[512,128]{1,0:T(8,128)(2,1)S(1)} %get-tuple-element.53), channel_id=1, source_target_pairs={{0,4},{4,0},{1,5},{5,1},{2,6},{6,2},{3,7},{7,3},{8,12},{12,8},{9,1... | collective-permute-start | bytes 393224 | tf_op jit(solution)/shard_map/ppermute | solution.py:374
  44.6 10.0 %collective-permute-start.3 = (bf16[256,512]{1,0:T(8,128)(2,1)S(1)}, bf16[256,512]{1,0:T(8,128)(2,1)S(1)}, u32[]{:S(2)}, u32[]{:S(2)}) collective-permute-start(bf16[256,512]{1,0:T(8,128)(2,1)S(1)} %get-tuple-element.70), channel_id=1, source_target_pairs={{0,3},{1,0},{2,1},{3,2},{4,7},{5,4},{6,5},{7,6},{8,11},{9,8},{10,9... | collective-permute-start | bytes 786440 | tf_op jit(solution)/shard_map/ppermute | solution.py:395
  47.9 8.5 %collective-permute-start.2 = (bf16[256,512]{1,0:T(8,128)(2,1)S(1)}, bf16[256,512]{1,0:T(8,128)(2,1)S(1)}, u32[]{:S(2)}, u32[]{:S(2)}) collective-permute-start(bf16[256,512]{1,0:T(8,128)(2,1)S(1)} %get-tuple-element.69), channel_id=1, source_target_pairs={{0,1},{1,2},{2,3},{3,0},{4,5},{5,6},{6,7},{7,4},{8,9},{9,10},{10,1... | collective-permute-start | bytes 786440 | tf_op jit(solution)/shard_map/ppermute | solution.py:391
  49.7 12.3 %collective-permute-start.5 = (bf16[256,512]{1,0:T(8,128)(2,1)S(1)}, bf16[256,512]{1,0:T(8,128)(2,1)S(1)}, u32[]{:S(2)}, u32[]{:S(2)}) collective-permute-start(bf16[256,512]{1,0:T(8,128)(2,1)S(1)} %get-tuple-element.72), channel_id=1, source_target_pairs={{0,1},{1,2},{2,3},{3,0},{4,5},{5,6},{6,7},{7,4},{8,9},{9,10},{10,1... | collective-permute-start | bytes 786440 | tf_op jit(solution)/shard_map/ppermute | solution.py:406
  49.8 12.2 %collective-permute-start.6 = (bf16[256,512]{1,0:T(8,128)(2,1)S(1)}, bf16[256,512]{1,0:T(8,128)(2,1)S(1)}, u32[]{:S(2)}, u32[]{:S(2)}) collective-permute-start(bf16[256,512]{1,0:T(8,128)(2,1)S(1)} %get-tuple-element.73), channel_id=1, source_target_pairs={{0,3},{1,0},{2,1},{3,2},{4,7},{5,4},{6,5},{7,6},{8,11},{9,8},{10,9... | collective-permute-start | bytes 786440 | tf_op jit(solution)/shard_map/ppermute | solution.py:407
  56.5 11.1 %collective-permute-start.4 = (bf16[256,512]{1,0:T(8,128)(2,1)S(1)}, bf16[256,512]{1,0:T(8,128)(2,1)S(1)}, u32[]{:S(2)}, u32[]{:S(2)}) collective-permute-start(bf16[256,512]{1,0:T(8,128)(2,1)S(1)} %get-tuple-element.71), channel_id=1, source_target_pairs={{0,1},{1,2},{2,3},{3,0},{4,5},{5,6},{6,7},{7,4},{8,9},{9,10},{10,1... | collective-permute-start | bytes 786440 | tf_op jit(solution)/shard_map/ppermute | solution.py:418
  56.6 11.1 %collective-permute-start.7 = (bf16[256,512]{1,0:T(8,128)(2,1)S(1)}, bf16[256,512]{1,0:T(8,128)(2,1)S(1)}, u32[]{:S(2)}, u32[]{:S(2)}) collective-permute-start(bf16[256,512]{1,0:T(8,128)(2,1)S(1)} %get-tuple-element.74), channel_id=1, source_target_pairs={{0,3},{1,0},{2,1},{3,2},{4,7},{5,4},{6,5},{7,6},{8,11},{9,8},{10,9... | collective-permute-start | bytes 786440 | tf_op jit(solution)/shard_map/ppermute | solution.py:419

commit v6 on v5

--- a/solution.py
+++ b/solution.py
@@ -82,53 +82,55 @@
     return columns(lax.rem(lax.axis_index("head") + shift, count), width)
 
 
-def swap_body(k_hbm, v_hbm, g_hbm, swap_ref, log_ref, state_ref, k_ref, v_ref, g_ref, sems):
-    half = DV // 2
-    theirs = v_hbm.at[:, columns(1 - lax.axis_index("core"), half)]
-    gate_copy, k_copy, v_copy = fetch(sems, (g_hbm, g_ref), (k_hbm, k_ref), (theirs, v_ref))
-    length = k_ref.shape[0]
-    mask = triangle(length, lambda r, c: c > r)
-    gate_copy.wait()
-    gate = g_ref[...]
-    after = dot(mask, gate)
-    total = after[0:1] + gate[0:1].astype(F32)
-    k_copy.wait()
-    v_copy.wait()
-    k_state = (k_ref[...].astype(F32) * jnp.exp(after)).astype(BF16)
-    state_ref[...] = k_state
-    state = dot(v_ref[...], k_state, ((0,), (0,))).astype(BF16)
-    swap_ref[0:half, :] = state[:, :LANE]
-    swap_ref[half : 2 * half, :] = state[:, LANE:]
-    left_high, left_low = split_bf16(total[:, :LANE])
-    right_high, right_low = split_bf16(total[:, LANE:])
-    tail = stacked(left_high, right_high, left_low, right_low)
-    swap_ref[2 * half :, :] = jnp.concatenate([tail, tail], axis=0).astype(BF16)
-    log_ref[...] = stacked(total[:, :LANE], total[:, LANE:])
-
-
-def own_body(v_hbm, state_ref, own_ref, v_ref, sems):
-    half = DV // 2
-    mine = v_hbm.at[:, columns(lax.axis_index("core"), half)]
-    (copy,) = fetch(sems, (mine, v_ref))
-    copy.wait()
-    state = dot(v_ref[...], state_ref[...], ((0,), (0,)))
-    own_ref[0:half, :] = state[:, :LANE]
-    own_ref[half:, :] = state[:, LANE:]
-
-
-def join_body(own_ref, log_ref, swap_ref, out_ref, first_ref, decay_ref):
+def state_body(
+    which, k_hbm, v_hbm, g_hbm, swap_ref, own_ref, log_ref, k_ref, v_ref, g_ref, sems
+):
+    @pl.when(lax.axis_index("core") == which)
+    def _():
+        gate_copy, k_copy, v_copy = fetch(sems, (g_hbm, g_ref), (k_hbm, k_ref), (v_hbm, v_ref))
+        length = k_ref.shape[0]
+        half = DV // 2
+        mask = triangle(length, lambda r, c: c > r)
+        gate_copy.wait()
+        gate = g_ref[...]
+        after = dot(mask, gate)
+        total = after[0:1] + gate[0:1].astype(F32)
+        k_copy.wait()
+        v_copy.wait()
+        k_state = (k_ref[...].astype(F32) * jnp.exp(after)).astype(BF16)
+        theirs, mine = (slice(at * half, (at + 1) * half) for at in (1 - which, which))
+        state = dot(v_ref[:, theirs], k_state, ((0,), (0,))).astype(BF16)
+        swap_ref[0:half, :] = state[:, :LANE]
+        swap_ref[half : 2 * half, :] = state[:, LANE:]
+        left_high, left_low = split_bf16(total[:, :LANE])
+        right_high, right_low = split_bf16(total[:, LANE:])
+        tail = stacked(left_high, right_high, left_low, right_low)
+        swap_ref[2 * half :, :] = jnp.concatenate([tail, tail], axis=0).astype(BF16)
+        state = dot(v_ref[:, mine], k_state, ((0,), (0,)))
+        own_ref[0:half, :] = state[:, :LANE]
+        own_ref[half:, :] = state[:, LANE:]
+        log_ref[...] = stacked(total[:, :LANE], total[:, LANE:])
+
+
+def join_body(
+    own_0_ref, log_0_ref, swap_0_ref, own_1_ref, log_1_ref, swap_1_ref,
+    out_ref, first_ref, decay_ref,
+):
     pieces, rows = (out_ref.shape[0], (out_ref.shape[1] - 8) // 2)
     half = pieces * rows
     early = lax.axis_index("core") == 0
-    tail = swap_ref[2 * half : 2 * half + 8, :].astype(F32)
+    swapped = jnp.where(early, swap_1_ref[...], swap_0_ref[...])
+    own_state = jnp.where(early, own_0_ref[...], own_1_ref[...])
+    logs = jnp.where(early, log_0_ref[...], log_1_ref[...])
+    tail = swapped[2 * half : 2 * half + 8].astype(F32)
     sums = []
     decays = []
     for side in range(2):
         at = slice(side * half, (side + 1) * half)
-        own_log = log_ref[side : side + 1, :]
+        own_log = logs[side : side + 1]
         other_log = tail[side : side + 1] + tail[side + 2 : side + 3]
-        own = own_ref[at, :]
-        other = swap_ref[at, :].astype(F32)
+        own = own_state[at]
+        other = swapped[at].astype(F32)
         first = jnp.where(early, own, other)
         second = jnp.where(early, other, own)
         state = first * jnp.exp(jnp.where(early, other_log, own_log)) + second
@@ -287,21 +289,18 @@
     down_out_ref[...] = (down_ref[...] + far_down_ref[...].astype(F32)).astype(BF16)
 
 
-CHUNKS = 4
-
-
 def sum_body(own_ref, below_a_ref, below_b_ref, above_a_ref, above_b_ref, out_hbm, out_ref, sems):
-    length, half = (own_ref.shape[0], below_a_ref.shape[0])
-    size = length // CHUNKS
+    split = below_a_ref.shape[0]
     copies = []
-    for i in range(CHUNKS):
-        at, start = slice(i * size, (i + 1) * size), i * size % half
-        part = slice(start, start + size)
-        below, above = (below_a_ref, above_a_ref) if i * size < half else (below_b_ref, above_b_ref)
-        total = own_ref[at, :] + below[part, :].astype(F32) + above[part, :].astype(F32)
+    for i, (at, below, above) in enumerate(
+        (
+            (slice(0, split), below_a_ref, above_a_ref),
+            (slice(split, own_ref.shape[0]), below_b_ref, above_b_ref),
+        )
+    ):
+        total = own_ref[at, :] + below[...].astype(F32) + above[...].astype(F32)
         out_ref[at, :] = total.astype(BF16)
-        copies.append(pltpu.make_async_copy(out_ref.at[at], out_hbm.at[at], sems.at[i]))
-        copies[-1].start()
+        copies += fetch(sems.at[pl.ds(i, 1)], (out_ref.at[at], out_hbm.at[at]))
     for copy in copies:
         copy.wait()
 
@@ -319,32 +318,24 @@
     width = out_weight.shape[1] // lax.axis_size("head")
     shape = jax.ShapeDtypeStruct
     small = shape((8, LANE), F32)
-    swap, own_log, k_state = call(
-        swap_body,
-        (shape((DV + 16, LANE), BF16), small, shape((length, DK), BF16)),
-        key_vectors,
-        values,
-        log_gate,
-        fetched=(0, 1, 2),
-        scratch=[pltpu.VMEM((length, n), BF16) for n in (DK, half, DK)],
-        copies=3,
-    )
-    swapped = lax.ppermute(swap, "core", ring("core", 1))
-    own = call(
-        own_body,
-        shape((DV, LANE), F32),
-        values,
-        k_state,
-        fetched=(0,),
-        scratch=[pltpu.VMEM((length, half), BF16)],
-        copies=1,
-    )
+    state_out = (shape((DV + 16, LANE), BF16), shape((DV, LANE), F32), small)
+    states = []
+    for core in (1, 0):
+        swap, own, own_log = call(
+            functools.partial(state_body, core),
+            state_out,
+            key_vectors,
+            values,
+            log_gate,
+            fetched=(0, 1, 2),
+        )
+        swap = lax.ppermute(swap, "core", [(core, 1 - core)])
+        states.append((own, own_log, swap))
     sent, early, decay = call(
         join_body,
         (shape((pieces, 2 * rows + 8, LANE), BF16), shape((DV, LANE), BF16), small),
-        own,
-        own_log,
-        swapped,
+        *states[1],
+        *states[0],
     )
     slices = lax.all_to_all(sent, CHIPS, 0, 0, tiled=True)
     prefixes = call(scan_body, shape((pieces, 2 * rows, LANE), BF16), slices)
@@ -373,8 +364,8 @@
     keep, send = call(part_body, (state_half, state_half), entering, early, decay)
     other = lax.ppermute(send, "core", ring("core", 1))
     column = shape((length, 1), F32)
-    near = shape((length // 2, width), BF16)
-    near_f = shape((length // 2, width), F32)
+    split = length // 2 + length // 32
+    tops, lows = shape((split, width), BF16), shape((length - split, width), BF16)
     kept, square, kept_far = call(
         keep_body,
         (shape((length, half), BF16), column, shape((length, width), F32)),
@@ -385,18 +376,17 @@
         w_far,
     )
     up, down = ring("head", 1), ring("head", -1)
-    rows_out = (shape((length // 2, DV), BF16), shape((length // 2, 1), F32), near)
+    rows_out = [(shape((n, DV), BF16), shape((n, 1), F32), shape((n, width), BF16))
+                for n in (split, length - split)]
     finish_in = (other, q_start, att_local, kept, square, kept_far, scale, w_far)
-    top, norm_top, far_up = call(functools.partial(finish_body, 0), rows_out, *finish_in)
+    top, norm_top, far_up = call(functools.partial(finish_body, 0), rows_out[0], *finish_in)
     far_up = lax.ppermute(far_up, "head", up)
-    low, norm_low, far_down = call(
-        functools.partial(finish_body, length // 2), rows_out, *finish_in
-    )
+    low, norm_low, far_down = call(functools.partial(finish_body, split), rows_out[1], *finish_in)
     far_down = lax.ppermute(far_down, "head", down)
     gated = (top, low, norm_top, norm_low)
     up_b, down_a = call(
         direct_body,
-        (near, near),
+        (lows, tops),
         *gated,
         out_weight,
         fetched=(4,),
@@ -407,14 +397,14 @@
     above_a = lax.ppermute(down_a, "head", down)
     up_a, down_b, own_part = call(
         near_body,
-        (near_f, near_f, shape((length, width), F32)),
+        (shape(tops.shape, F32), shape(lows.shape, F32), shape((length, width), F32)),
         *gated,
         out_weight,
         fetched=(4,),
         scratch=[pltpu.VMEM((3, DV, width), BF16)],
         copies=3,
     )
-    up_a, down_b = call(pass_body, (near, near), up_a, down_b, far_up, far_down)
+    up_a, down_b = call(pass_body, (tops, lows), up_a, down_b, far_up, far_down)
     below_a = lax.ppermute(up_a, "head", up)
     above_b = lax.ppermute(down_b, "head", down)
     return call(
@@ -426,7 +416,7 @@
         above_a,
         above_b,
         scratch=[pltpu.VMEM((length, width), BF16)],
-        copies=CHUNKS,
+        copies=2,
         outs_in=HBM,
     )
 

time: 68.8 us -> 71.7 us (1.042)
  the two profiles are of different devices: /device:TPU:1 before, /device:TPU:24 now
where the time goes in v6:
time: 71.7 us; the launch traced here: 70.6 us
  blocking collectives  22.8 us (32%)
  waiting for transfers between devices  21.3 us (30%)
  Pallas kernels  14.1 us (20%)
  starting transfers between devices  12.2 us (17%)
    all_to_all x1, blocking collectives, shards(): slices = lax.all_to_all(sent, CHIPS, 0, 0, tiled=True)  22.8 us
    pallas_call x13, Pallas kernels, call(): pl.pallas_call(body, out_shape=outs, in_specs=[HBM if i in fetched else V...  14.1 us
    ppermute x1, waiting for transfers between devices, shards(): below_b = lax.ppermute(up_b, 'head', up)  9.47 us
    all_to_all x1, waiting for transfers between devices, shards(): entering = lax.all_to_all(prefixes, CHIPS, 0, 0, tiled=True)  5.61 us
    all_to_all x1, starting transfers between devices, shards(): entering = lax.all_to_all(prefixes, CHIPS, 0, 0, tiled=True)  4.09 us
    ppermute x1, waiting for transfers between devices, shards(): far_down = lax.ppermute(far_down, 'head', down)  3.62 us
    ppermute x2, starting transfers between devices, shards(): swap = lax.ppermute(swap, 'core', [(core, 1 - core)])  2.59 us
    ppermute x2, waiting for transfers between devices, shards(): swap = lax.ppermute(swap, 'core', [(core, 1 - core)])  1.94 us
  transfers between devices with their start and end apart: 10, of which 5 were waited for; matrix products, arithmetic and copies ran while one was open for 0% of the time, Pallas kernels for 14%

profile of v6, /device:TPU:24, one launch (start us, length us, event | category | flops | bytes accessed | tf_op | source)
XLA Modules:
  0.0 70.6 jit_solution(2278202922703159880)
XLA Ops:
  0.0 1.8 %shard_map.73 = (bf16[528,128]{1,0:T(8,128)(2,1)S(1)}, f32[512,128]{1,0:T(8,128)S(1)}, f32[8,128]{1,0:T(8,128)S(1)}) custom-call(bf16[512,256]{1,0:T(8,128)(2,1)} %k_hbm.5, bf16[512,512]{1,0:T(8,128)(2,1)} %v_hbm.5, bf16[512,256]{1,0:T(8,128)(2,1)} %g_hbm.5), custom_call_target="tpu_custom_call" | custom-call | flops 1000000000 | bytes 1048576 | tf_op jit(solution)/shard_map/pallas_call | solution.py:35
  1.9 1.3 %collective-permute-start = (bf16[528,128]{1,0:T(8,128)(2,1)S(1)}, bf16[528,128]{1,0:T(8,128)(2,1)S(1)}, u32[]{:S(2)}, u32[]{:S(2)}) collective-permute-start(bf16[528,128]{1,0:T(8,128)(2,1)S(1)} %get-tuple-element.45), channel_id=1, source_target_pairs={{0,4},{1,5},{2,6},{3,7},{8,12},{9,13},{10,14},{11,15},{16,20},{17,... | collective-permute-start | bytes 405512 | tf_op jit(solution)/shard_map/ppermute | solution.py:332
  3.2 1.3 %collective-permute-start.1 = (bf16[528,128]{1,0:T(8,128)(2,1)S(1)}, bf16[528,128]{1,0:T(8,128)(2,1)S(1)}, u32[]{:S(2)}, u32[]{:S(2)}) collective-permute-start(bf16[528,128]{1,0:T(8,128)(2,1)S(1)} %get-tuple-element.48), channel_id=1, source_target_pairs={{4,0},{5,1},{6,2},{7,3},{12,8},{13,9},{14,10},{15,11},{20,16},{21,... | collective-permute-start | bytes 405512 | tf_op jit(solution)/shard_map/ppermute | solution.py:332
  4.5 1.9 %collective-permute-done.1.swap_1_ref = bf16[528,128]{1,0:T(8,128)(2,1)S(1)} collective-permute-done((bf16[528,128]{1,0:T(8,128)(2,1)S(1)}, bf16[528,128]{1,0:T(8,128)(2,1)S(1)}, u32[]{:S(2)}, u32[]{:S(2)}) %collective-permute-start.1) | collective-permute-done | bytes 135200 | tf_op jit(solution)/shard_map/ppermute | solution.py:332
  6.6 22.8 %all_to_all.10.in_ref = bf16[32,24,128]{2,1,0:T(8,128)(2,1)S(1)} all-to-all(bf16[32,24,128]{2,1,0:T(8,128)(2,1)S(1)} %get-tuple-element.49), channel_id=1, replica_groups=mesh['chip_x'=4,'chip_z'=8,'core'=2,'head'=4] {'chip_x','chip_z'}, dimensions={0} | all-to-all | bytes 393216 | tf_op jit(solution)/shard_map/all_to_all | solution.py:340
  29.4 0.7 %shard_map.76 = bf16[32,16,128]{2,1,0:T(8,128)(2,1)} custom-call(bf16[32,24,128]{2,1,0:T(8,128)(2,1)S(1)} %all_to_all.10.in_ref), custom_call_target="tpu_custom_call" | custom-call | flops 1000000000 | bytes 196608 | tf_op jit(solution)/shard_map/pallas_call | solution.py:35
  30.1 4.1 %all-to-all-start.1 = ((bf16[32,16,128]{2,1,0:T(8,128)(2,1)}), bf16[32,16,128]{2,1,0:T(8,128)(2,1)S(1)}, u32[]{:S(2)}, u32[]{:S(2)}) async-start(bf16[32,16,128]{2,1,0:T(8,128)(2,1)} %shard_map.76), calls=%async_computation.1 | async-start | bytes 262144 | tf_op jit(solution)/shard_map/all_to_all | solution.py:359
  34.2 4.8 %shard_map.77 = (f32[512,512]{1,0:T(8,128)S(1)}, bf16[512,256]{1,0:T(8,128)(2,1)S(1)}, bf16[512,512]{1,0:T(8,128)(2,1)S(1)}, bf16[512,512]{1,0:T(8,128)(2,1)S(1)}) custom-call(bf16[512,256]{1,0:T(8,128)(2,1)} %q_hbm, bf16[512,256]{1,0:T(8,128)(2,1)} %k_hbm.5, bf16[512,512]{1,0:T(8,128)(2,1)} %v_hbm.5, bf16[512,256]{1,0:T(8,128)(2,1)} %g_hbm.5, ...), custom_call_target="tpu_custom_call" | custom-call | flops 1000000000 | bytes 3934208 | tf_op jit(solution)/shard_map/pallas_call | solution.py:35
  39.0 5.6 %all-to-all-done.1.in_ref = bf16[32,16,128]{2,1,0:T(8,128)(2,1)S(1)} async-done(((bf16[32,16,128]{2,1,0:T(8,128)(2,1)}), bf16[32,16,128]{2,1,0:T(8,128)(2,1)S(1)}, u32[]{:S(2)}, u32[]{:S(2)}) %all-to-all-start.1) | async-done | bytes 131104 | tf_op jit(solution)/shard_map/all_to_all | solution.py:359
  44.8 0.7 shard_map.79
  45.5 0.7 collective-permute-done.2.other_ref
  46.2 0.5 shard_map.80
  46.7 0.3 collective-permute-start.3
  47.0 0.5 shard_map.81
  47.5 1.9 %collective-permute-start.4 = (bf16[240,512]{1,0:T(8,128)(2,1)S(1)}, bf16[240,512]{1,0:T(8,128)(2,1)S(1)}, u32[]{:S(2)}, u32[]{:S(2)}) collective-permute-start(bf16[240,512]{1,0:T(8,128)(2,1)S(1)} %get-tuple-element.76), channel_id=1, source_target_pairs={{0,3},{1,0},{2,1},{3,2},{4,7},{5,4},{6,5},{7,6},{8,11},{9,8},{10,9... | collective-permute-start | bytes 737288 | tf_op jit(solution)/shard_map/ppermute | solution.py:385
  49.4 1.7 %shard_map.84 = (bf16[240,512]{1,0:T(8,128)(2,1)S(1)}, bf16[272,512]{1,0:T(8,128)(2,1)S(1)}) custom-call(bf16[272,512]{1,0:T(8,128)(2,1)S(1)} %get-tuple-element.68.top_ref, bf16[240,512]{1,0:T(8,128)(2,1)S(1)} %get-tuple-element.69.low_ref, f32[272,1]{1,0:T(8,128)S(1)} %get-tuple-element.70.norm_top_ref, f32[240,1]{1,0:T(8,128)S(1)} %get-tuple-element.71.norm_low_ref, ...), custom_call_target="tpu_custom_call" | custom-call | flops 1000000000 | bytes 2623488 | tf_op jit(solution)/shard_map/pallas_call | solution.py:35
  51.0 0.8 %collective-permute-start.7 = (bf16[272,512]{1,0:T(8,128)(2,1)S(1)}, bf16[272,512]{1,0:T(8,128)(2,1)S(1)}, u32[]{:S(2)}, u32[]{:S(2)}) collective-permute-start(bf16[272,512]{1,0:T(8,128)(2,1)S(1)} %get-tuple-element.79), channel_id=1, source_target_pairs={{0,3},{1,0},{2,1},{3,2},{4,7},{5,4},{6,5},{7,6},{8,11},{9,8},{10,9... | collective-permute-start | bytes 835592 | tf_op jit(solution)/shard_map/ppermute | solution.py:397
  51.9 2.1 %shard_map.82 = (f32[272,512]{1,0:T(8,128)S(1)}, f32[240,512]{1,0:T(8,128)S(1)}, f32[512,512]{1,0:T(8,128)S(1)}) custom-call(bf16[272,512]{1,0:T(8,128)(2,1)S(1)} %get-tuple-element.68.top_ref, bf16[240,512]{1,0:T(8,128)(2,1)S(1)} %get-tuple-element.69.low_ref, f32[272,1]{1,0:T(8,128)S(1)} %get-tuple-element.70.norm_top_ref, ...), custom_call_target="tpu_custom_call" | custom-call | flops 1000000000 | bytes 2623488 | tf_op jit(solution)/shard_map/pallas_call | solution.py:35
  54.0 3.6 %collective-permute-done.4.far_down_ref = bf16[240,512]{1,0:T(8,128)(2,1)S(1)} collective-permute-done((bf16[240,512]{1,0:T(8,128)(2,1)S(1)}, bf16[240,512]{1,0:T(8,128)(2,1)S(1)}, u32[]{:S(2)}, u32[]{:S(2)}) %collective-permute-start.4) | collective-permute-done | bytes 245792 | tf_op jit(solution)/shard_map/ppermute | solution.py:385
  57.7 0.4 collective-permute-start.5
  58.1 1.6 %collective-permute-start.6 = (bf16[240,512]{1,0:T(8,128)(2,1)S(1)}, bf16[240,512]{1,0:T(8,128)(2,1)S(1)}, u32[]{:S(2)}, u32[]{:S(2)}) collective-permute-start(bf16[240,512]{1,0:T(8,128)(2,1)S(1)} %get-tuple-element.78), channel_id=1, source_target_pairs={{0,1},{1,2},{2,3},{3,0},{4,5},{5,6},{6,7},{7,4},{8,9},{9,10},{10,1... | collective-permute-start | bytes 737288 | tf_op jit(solution)/shard_map/ppermute | solution.py:396
  59.7 0.4 collective-permute-start.8
  60.2 9.5 %collective-permute-done.6.below_b_ref = bf16[240,512]{1,0:T(8,128)(2,1)S(1)} collective-permute-done((bf16[240,512]{1,0:T(8,128)(2,1)S(1)}, bf16[240,512]{1,0:T(8,128)(2,1)S(1)}, u32[]{:S(2)}, u32[]{:S(2)}) %collective-permute-start.6) | collective-permute-done | bytes 245792 | tf_op jit(solution)/shard_map/ppermute | solution.py:396
  69.7 0.9 %shard_map.85 = bf16[512,512]{1,0:T(8,128)(2,1)} custom-call(f32[512,512]{1,0:T(8,128)S(1)} %get-tuple-element.72.own_ref, bf16[272,512]{1,0:T(8,128)(2,1)S(1)} %collective-permute-done.5.below_a_ref, bf16[240,512]{1,0:T(8,128)(2,1)S(1)} %collective-permute-done.6.below_b_ref, bf16[272,512]{1,0:T(8,128)(2,1)S(1)} %collective-permute-done.7.above_a_ref, ...), custom_call_target="tpu_custom_call" | custom-call | flops 1000000000 | bytes 2097152 | tf_op jit(solution)/shard_map/pallas_call | solution.py:35
  (12 shorter events, 0.4 us)
Async XLA Ops:
  1.9 2.7 %collective-permute-start = (bf16[528,128]{1,0:T(8,128)(2,1)S(1)}, bf16[528,128]{1,0:T(8,128)(2,1)S(1)}, u32[]{:S(2)}, u32[]{:S(2)}) collective-permute-start(bf16[528,128]{1,0:T(8,128)(2,1)S(1)} %get-tuple-element.45), channel_id=1, source_target_pairs={{0,4},{1,5},{2,6},{3,7},{8,12},{9,13},{10,14},{11,15},{16,20},{17,... | collective-permute-start | bytes 405512 | tf_op jit(solution)/shard_map/ppermute | solution.py:332
  3.2 3.2 %collective-permute-start.1 = (bf16[528,128]{1,0:T(8,128)(2,1)S(1)}, bf16[528,128]{1,0:T(8,128)(2,1)S(1)}, u32[]{:S(2)}, u32[]{:S(2)}) collective-permute-start(bf16[528,128]{1,0:T(8,128)(2,1)S(1)} %get-tuple-element.48), channel_id=1, source_target_pairs={{4,0},{5,1},{6,2},{7,3},{12,8},{13,9},{14,10},{15,11},{20,16},{21,... | collective-permute-start | bytes 405512 | tf_op jit(solution)/shard_map/ppermute | solution.py:332
  6.6 27.6 %copy-start = (f32[512]{0:T(512)S(1)}, f32[512]{0:T(512)}, u32[]{:S(2)}) copy-start(f32[512]{0:T(512)} %param.12) | copy-start | bytes 6148
  30.1 14.5 %all-to-all-start.1 = ((bf16[32,16,128]{2,1,0:T(8,128)(2,1)}), bf16[32,16,128]{2,1,0:T(8,128)(2,1)S(1)}, u32[]{:S(2)}, u32[]{:S(2)}) async-start(bf16[32,16,128]{2,1,0:T(8,128)(2,1)} %shard_map.76), calls=%async_computation.1 | async-start | bytes 262144 | tf_op jit(solution)/shard_map/all_to_all | solution.py:359
  44.7 1.4 %collective-permute-start.2 = (bf16[512,128]{1,0:T(8,128)(2,1)S(1)}, bf16[512,128]{1,0:T(8,128)(2,1)S(1)}, u32[]{:S(2)}, u32[]{:S(2)}) collective-permute-start(bf16[512,128]{1,0:T(8,128)(2,1)S(1)} %get-tuple-element.59), channel_id=1, source_target_pairs={{0,4},{4,0},{1,5},{5,1},{2,6},{6,2},{3,7},{7,3},{8,12},{12,8},{9,1... | collective-permute-start | bytes 393224 | tf_op jit(solution)/shard_map/ppermute | solution.py:365
  46.7 10.9 %collective-permute-start.3 = (bf16[272,512]{1,0:T(8,128)(2,1)S(1)}, bf16[272,512]{1,0:T(8,128)(2,1)S(1)}, u32[]{:S(2)}, u32[]{:S(2)}) collective-permute-start(bf16[272,512]{1,0:T(8,128)(2,1)S(1)} %get-tuple-element.75), channel_id=1, source_target_pairs={{0,1},{1,2},{2,3},{3,0},{4,5},{5,6},{6,7},{7,4},{8,9},{9,10},{10,1... | collective-permute-start | bytes 835592 | tf_op jit(solution)/shard_map/ppermute | solution.py:383
  47.5 10.1 %collective-permute-start.4 = (bf16[240,512]{1,0:T(8,128)(2,1)S(1)}, bf16[240,512]{1,0:T(8,128)(2,1)S(1)}, u32[]{:S(2)}, u32[]{:S(2)}) collective-permute-start(bf16[240,512]{1,0:T(8,128)(2,1)S(1)} %get-tuple-element.76), channel_id=1, source_target_pairs={{0,3},{1,0},{2,1},{3,2},{4,7},{5,4},{6,5},{7,6},{8,11},{9,8},{10,9... | collective-permute-start | bytes 737288 | tf_op jit(solution)/shard_map/ppermute | solution.py:385
  51.0 18.6 %collective-permute-start.7 = (bf16[272,512]{1,0:T(8,128)(2,1)S(1)}, bf16[272,512]{1,0:T(8,128)(2,1)S(1)}, u32[]{:S(2)}, u32[]{:S(2)}) collective-permute-start(bf16[272,512]{1,0:T(8,128)(2,1)S(1)} %get-tuple-element.79), channel_id=1, source_target_pairs={{0,3},{1,0},{2,1},{3,2},{4,7},{5,4},{6,5},{7,6},{8,11},{9,8},{10,9... | collective-permute-start | bytes 835592 | tf_op jit(solution)/shard_map/ppermute | solution.py:397
  57.7 12.0 %collective-permute-start.5 = (bf16[272,512]{1,0:T(8,128)(2,1)S(1)}, bf16[272,512]{1,0:T(8,128)(2,1)S(1)}, u32[]{:S(2)}, u32[]{:S(2)}) collective-permute-start(bf16[272,512]{1,0:T(8,128)(2,1)S(1)} %get-tuple-element.77), channel_id=1, source_target_pairs={{0,1},{1,2},{2,3},{3,0},{4,5},{5,6},{6,7},{7,4},{8,9},{9,10},{10,1... | collective-permute-start | bytes 835592 | tf_op jit(solution)/shard_map/ppermute | solution.py:408
  58.1 11.5 %collective-permute-start.6 = (bf16[240,512]{1,0:T(8,128)(2,1)S(1)}, bf16[240,512]{1,0:T(8,128)(2,1)S(1)}, u32[]{:S(2)}, u32[]{:S(2)}) collective-permute-start(bf16[240,512]{1,0:T(8,128)(2,1)S(1)} %get-tuple-element.78), channel_id=1, source_target_pairs={{0,1},{1,2},{2,3},{3,0},{4,5},{5,6},{6,7},{7,4},{8,9},{9,10},{10,1... | collective-permute-start | bytes 737288 | tf_op jit(solution)/shard_map/ppermute | solution.py:396
  59.7 9.9 %collective-permute-start.8 = (bf16[240,512]{1,0:T(8,128)(2,1)S(1)}, bf16[240,512]{1,0:T(8,128)(2,1)S(1)}, u32[]{:S(2)}, u32[]{:S(2)}) collective-permute-start(bf16[240,512]{1,0:T(8,128)(2,1)S(1)} %get-tuple-element.80), channel_id=1, source_target_pairs={{0,3},{1,0},{2,1},{3,2},{4,7},{5,4},{6,5},{7,6},{8,11},{9,8},{10,9... | collective-permute-start | bytes 737288 | tf_op jit(solution)/shard_map/ppermute | solution.py:409
